TPU v7x, 512 devices: a whole 4x4x16 slice. The times are simulated.
512 devices in a mesh: dp: 4 (over y), seq: 16 (over z), tensor: 8 (over x, core).
Axes of the slice: x: 4, y: 4, z: 16, core: 2. Of those that a mesh axis runs over, the one named last changes fastest.
Arguments:
- queries: bfloat16 [4, 1024, 8192], P('dp', 'seq', 'tensor'), may hold values from -6 to 6
- new_keys: bfloat16 [4, 1024, 1024], P('dp', 'seq', 'tensor'), may hold values from -6 to 6
- new_values: bfloat16 [4, 1024, 1024], P('dp', 'seq', 'tensor'), may hold values from -6 to 6
- cache_keys: bfloat16 [4, 8192, 1024], P('dp', 'seq', 'tensor'), may hold values from -6 to 6
- cache_values: bfloat16 [4, 8192, 1024], P('dp', 'seq', 'tensor'), may hold values from -6 to 6
- keep_lengths: int32 [4, 16], P('dp', 'seq'), may hold values from 1 to 512
- cache_doc: int32 [4, 8192], P('dp', 'seq'), may hold values from 0 to 1
- new_doc: int32 [4, 1024], P('dp', 'seq'), may hold values from 0 to 1, never falling along the last dimension, each value on 1 to 640 neighbouring positions
- out_weight: bfloat16 [8192, 8192], P('tensor', 'dp'), may hold values from -0.0625 to 0.0625
Outputs:
- mixed_out: bfloat16 [4, 1024, 4, 2048], P('dp', 'seq', None, 'tensor')
Inputs may be any that keep to these rules, and one draw needn't show every extreme that they name: `keep_lengths`: valid cache rows of a shard come first. `cache_doc`: documents 0 and 1 of the pack. `new_doc`: never falling along the tokens of a pack; both documents present.
All inputs are finite; a program needn't handle non-finite values.
Results may differ from a plain program's by a relative error of at most 0.0056.
Values may be sent and summed in bfloat16 or wider, within the bound.
No kernel may reach another device: no remote copies, remote signals or barrier semaphores. Data moves between devices by JAX's collectives and lax.ppermute only.
A program may use at most 128 MiB of HBM per device.

v0:
```python
import math

import jax
import jax.numpy as jnp
from jax import lax
from jax.sharding import PartitionSpec as P

HD = 128


masked_score = -1e30


def in_one_piece(arrays, axis, dim, along):
    ends, at = ([], 0)
    for a in arrays[:-1]:
        at += a.shape[along]
        ends.append(at)
    both = jnp.concatenate(arrays, axis=along)
    return tuple(jnp.split(lax.all_gather(both, axis, axis=dim, tiled=True), ends, axis=along))


def in_order(parts, dim):
    shape = list(parts.shape[1:])
    shape[dim] *= parts.shape[0]
    return jnp.moveaxis(parts, 0, dim).reshape(shape)


def copy_for_each(x, axis):
    copies = jnp.broadcast_to(x, (lax.axis_size(axis), *x.shape))
    return lax.all_to_all(copies, axis, split_axis=0, concat_axis=0, tiled=True)


def gathered_copies(x, axis, dim):
    return in_order(copy_for_each(x, axis), dim)


def split_up(x, dim, size):
    shape = x.shape
    parts = x.reshape(*shape[:dim], size, shape[dim] // size, *shape[dim + 1 :])
    return jnp.moveaxis(parts, dim, 0)


def summed_on_arrival(x, axis, dim):
    parts = split_up(x, dim, lax.axis_size(axis))
    arrived = lax.all_to_all(parts, axis, split_axis=0, concat_axis=0, tiled=True)
    return arrived.sum(axis=0)


def softmax_terms(scores, visible, value_rows):
    scores = jnp.where(visible, scores, masked_score)
    top_score = jnp.max(scores, axis=-1)
    weights = jnp.where(visible, jnp.exp(scores - top_score[..., None]), 0.0)
    weight_sum = jnp.sum(weights, axis=-1)
    summed = jnp.dot(weights.astype(jnp.bfloat16), value_rows, preferred_element_type=jnp.float32)
    return (top_score, weight_sum, summed)


def masked_terms(query_rows, row_doc, key_rows, value_rows, doc_rows, length, score_scale):
    scores = jnp.dot(query_rows, key_rows.T, preferred_element_type=jnp.float32) * score_scale
    positions = jnp.arange(key_rows.shape[0], dtype=jnp.int32)
    visible = (positions[None, :] < length) & (doc_rows[None, :] == row_doc[:, None])
    return softmax_terms(scores, visible, value_rows)


def join_terms(earlier, later):
    top_score = jnp.maximum(earlier[0], later[0])
    early_factor = jnp.exp(earlier[0] - top_score)
    late_factor = jnp.exp(later[0] - top_score)
    weight_sum = earlier[1] * early_factor + later[1] * late_factor
    summed = earlier[2] * early_factor[..., None] + later[2] * late_factor[..., None]
    return (top_score, weight_sum, summed)


def local(
    queries,
    new_keys,
    new_values,
    cache_keys,
    cache_values,
    keep_lengths,
    cache_doc,
    new_doc,
    out_weight,
):
    score_scale = HD ** (-0.5)
    tok_rows = queries.shape[1]
    local_heads = queries.shape[2] // HD
    local_kv = cache_keys.shape[2] // HD
    head_group = local_heads // local_kv
    cache_rows = cache_keys.shape[1]
    all_queries, all_keys, all_values, all_doc = (
        *in_one_piece((queries, new_keys, new_values), "seq", 1, 2),
        lax.all_gather(new_doc, "seq", axis=1, tiled=True),
    )
    pack_len = all_queries.shape[1]
    query_rows = all_queries[0].reshape(pack_len, local_kv, head_group, HD).transpose(1, 0, 2, 3)
    row_doc = jnp.repeat(all_doc[0], head_group)
    block_size = math.gcd(pack_len * head_group, 1024)
    block_count = pack_len * head_group // block_size
    query_blocks = query_rows.reshape(local_kv * block_count, block_size, HD)
    doc_blocks = jnp.tile(row_doc.reshape(block_count, block_size), (local_kv, 1))
    head_ids = jnp.repeat(jnp.arange(local_kv, dtype=jnp.int32), block_count)
    key_heads = cache_keys[0].reshape(cache_rows, local_kv, HD).transpose(1, 0, 2)
    value_heads = cache_values[0].reshape(cache_rows, local_kv, HD).transpose(1, 0, 2)
    doc_rows = cache_doc[0]
    length = keep_lengths[0, 0]

    def block_terms(inputs):
        query_block, block_doc, head_index = inputs
        key_rows = lax.dynamic_index_in_dim(key_heads, head_index, 0, keepdims=False)
        value_rows = lax.dynamic_index_in_dim(value_heads, head_index, 0, keepdims=False)
        return masked_terms(
            query_block, block_doc, key_rows, value_rows, doc_rows, length, score_scale
        )

    block_tops, block_sums, block_partial = lax.map(
        block_terms, (query_blocks, doc_blocks, head_ids)
    )
    cache_top = block_tops.reshape(local_kv, pack_len, head_group)
    cache_sum = block_sums.reshape(local_kv, pack_len, head_group)
    cache_partial = block_partial.reshape(local_kv, pack_len, head_group, HD)
    my_start = lax.axis_index("seq") * tok_rows
    shares = (
        lax.all_to_all(cache_top[None], "seq", split_axis=2, concat_axis=0, tiled=True),
        lax.all_to_all(cache_sum[None], "seq", split_axis=2, concat_axis=0, tiled=True),
        lax.all_to_all(cache_partial[None], "seq", split_axis=2, concat_axis=0, tiled=True),
    )
    overall_top = jnp.max(shares[0], axis=0)
    factors = jnp.exp(shares[0] - overall_top[None])
    merged = (
        overall_top,
        jnp.sum(shares[1] * factors, 0),
        jnp.sum(shares[2] * factors[..., None], 0),
    )
    own_queries = (
        queries[0]
        .reshape(tok_rows, local_kv, head_group, HD)
        .transpose(1, 0, 2, 3)
        .reshape(local_kv, tok_rows * head_group, HD)
    )
    fresh_keys = all_keys[0].reshape(pack_len, local_kv, HD).transpose(1, 0, 2)
    fresh_values = all_values[0].reshape(pack_len, local_kv, HD).transpose(1, 0, 2)
    scores = (
        jnp.einsum("gqd,gkd->gqk", own_queries, fresh_keys, preferred_element_type=jnp.float32)
        * score_scale
    )
    row_token = my_start + jnp.arange(tok_rows * head_group, dtype=jnp.int32) // head_group
    own_doc = jnp.repeat(new_doc[0], head_group)
    key_index = jnp.arange(pack_len, dtype=jnp.int32)
    visible = (
        (key_index[None, :] <= row_token[:, None]) & (all_doc[0][None, :] == own_doc[:, None])
    )[None]
    scores = jnp.where(visible, scores, masked_score)
    fresh_top = jnp.max(scores, axis=-1)
    weights = jnp.where(visible, jnp.exp(scores - fresh_top[..., None]), 0.0)
    fresh_sum = jnp.sum(weights, axis=-1)
    fresh_partial = jnp.einsum(
        "gqk,gkd->gqd",
        weights.astype(jnp.bfloat16),
        fresh_values,
        preferred_element_type=jnp.float32,
    )
    fresh = (
        fresh_top.reshape(local_kv, tok_rows, head_group),
        fresh_sum.reshape(local_kv, tok_rows, head_group),
        fresh_partial.reshape(local_kv, tok_rows, head_group, HD),
    )
    final = join_terms(merged, fresh)
    attended = (
        (final[2] / final[1][..., None])
        .transpose(1, 0, 2, 3)
        .reshape(1, tok_rows, local_heads * HD)
        .astype(jnp.bfloat16)
    )
    partial_cols = jnp.einsum(
        "ptf,fc->ptc",
        gathered_copies(attended, "dp", 0),
        out_weight,
        preferred_element_type=jnp.float32,
    )
    summed_cols = summed_on_arrival(partial_cols, "tensor", 2).astype(jnp.bfloat16)
    return lax.all_to_all(summed_cols[:, :, None, :], "dp", split_axis=0, concat_axis=2, tiled=True)


def solution(mesh):
    placed = (
        P("dp", "seq", "tensor"),
        P("dp", "seq", "tensor"),
        P("dp", "seq", "tensor"),
        P("dp", "seq", "tensor"),
        P("dp", "seq", "tensor"),
        P("dp", "seq"),
        P("dp", "seq"),
        P("dp", "seq"),
        P("tensor", "dp"),
    )
    return jax.shard_map(
        local, mesh=mesh, in_specs=placed, out_specs=P("dp", "seq", None, "tensor"), check_vma=False
    )
```

profile of v0, /device:TPU:1, one launch (start us, length us, event | category | flops | bytes accessed | tf_op | source)
XLA Modules:
  0.0 413.9 jit_solution(15268883956794797267)
XLA Ops:
  10.9 23.8 %all-reduce = s32[1024]{0:T(1024)S(1)} all-reduce(s32[1024]{0:T(1024)S(1)} %bitcast_dynamic-update-slice_fusion), channel_id=1, replica_groups=mesh['dp'=4,'seq'=16,'tensor'=8] {'seq'}, use_global_device_ids=true, to_apply=%add | all-reduce | flops 1024 | bytes 8192
  35.2 44.3 %all-gather.2.cloned.1.call-done = bf16[1,1024,1280]{2,1,0:T(8,128)(2,1)} async-done(((bf16[1,64,1280]{2,1,0:T(8,128)(2,1)}), bf16[1,1024,1280]{2,1,0:T(8,128)(2,1)}) %all-gather.2.cloned.1.call-update) | async-done | bytes 2621456 | tf_op jit(solution)/shard_map/all_gather | solution.py:20
  81.1 2.3 reshape_transpose_reshape_squeeze.4
  83.4 38.9 %while.14 = (s32[]{:T(128)}, f32[8,1024]{1,0:T(8,128)S(1)}, f32[8,1024]{1,0:T(8,128)S(1)}, f32[8,1024,128]{2,1,0:T(8,128)}, s32[]{:T(128)}, /*index=5*/s32[1,512...) while((s32[]{:T(128)}, f32[8,1024]{1,0:T(8,128)S(1)}, ...), condition=%wide.region_3.4_spmd, body=%wide.region_0.3_spmd.sunk | while | flops 276298240 | bytes 7402629 | solution.py:117
  90.5 1.7 fusion.50
  100.3 1.7 fusion.50
  110.0 1.7 fusion.50
  119.8 1.7 fusion.50
  123.2 1.8 reduce.7
  125.9 6.5 %all-to-all-start.1 = ((f32[16,1,512]{2,1,0:T(1,128)}), f32[16,1,512]{2,1,0:T(1,128)S(1)}, u32[]{:S(2)}, u32[]{:S(2)}) async-start(f32[16,1,512]{2,1,0:T(1,128)} %reshape.252), calls=%async_computation.1 | async-start | bytes 65536 | tf_op jit(solution)/shard_map/all_to_all | solution.py:125
  132.7 1.8 reduce.9
  134.8 9.0 %all-to-all-done.1 = f32[16,1,512]{2,1,0:T(1,128)S(1)} async-done(((f32[16,1,512]{2,1,0:T(1,128)}), f32[16,1,512]{2,1,0:T(1,128)S(1)}, u32[]{:S(2)}, u32[]{:S(2)}) %all-to-all-start.1) | async-done | bytes 32800 | tf_op jit(solution)/shard_map/all_to_all | solution.py:125
  143.9 14.0 %all_to_all.67 = f32[16,1,512]{2,1,0:T(1,128)S(1)} all-to-all(f32[16,1,512]{2,1,0:T(1,128)S(1)} %reshape.254), channel_id=1, replica_groups=mesh['dp'=4,'seq'=16,'tensor'=8] {'seq'}, dimensions={0} | all-to-all | bytes 65536 | tf_op jit(solution)/shard_map/all_to_all | solution.py:126
  157.9 5.0 %all-to-all-start = ((f32[1,1,1024,8,128]{4,3,1,0,2:T(8,128)}), f32[1,1,1024,8,128]{4,3,1,0,2:T(8,128)}, u32[]{:S(2)}, u32[]{:S(2)}) async-start(f32[1,1,1024,8,128]{4,3,1,0,2:T(8,128)} %bitcast.110), calls=%async_computation | async-start | bytes 8388608 | tf_op jit(solution)/shard_map/all_to_all | solution.py:127
  163.1 2.0 fusion.15
  165.2 2.4 fusion.19
  169.9 1.7 reshape.255
  173.7 169.8 %all-to-all-done = f32[1,1,1024,8,128]{4,3,1,0,2:T(8,128)} async-done(((f32[1,1,1024,8,128]{4,3,1,0,2:T(8,128)}), f32[1,1,1024,8,128]{4,3,1,0,2:T(8,128)}, u32[]{:S(2)}, u32[]{:S(2)}) %all-to-all-start) | async-done | bytes 4194336 | tf_op jit(solution)/shard_map/all_to_all | solution.py:127
  343.5 3.1 multiply_reduce_fusion
  348.3 4.1 all-to-all-start.3
  352.4 6.4 %copy.20 = bf16[2048,1024]{1,0:T(8,128)(2,1)} copy(bf16[2048,1024]{0,1:T(8,128)(2,1)} %bitcast.109) | data formatting | bytes 8388608 | tf_op jit(solution)/shard_map/ptf,fc->ptc/dot_general | solution.py:176
  359.4 3.5 convolution_bitcast_fusion.1
  363.1 35.6 %all_to_all.68 = f32[8,4,64,256]{3,2,1,0:T(8,128)S(1)} all-to-all(f32[8,4,64,256]{3,2,1,0:T(8,128)S(1)} %copy.15), channel_id=1, replica_groups=mesh['dp'=4,'seq'=16,'tensor'=8] {'tensor'}, dimensions={0} | all-to-all | bytes 4194304 | tf_op jit(solution)/shard_map/all_to_all | solution.py:46
  398.8 7.5 %all_to_all.69 = bf16[4,64,1,256]{3,1,2,0:T(8,128)(2,1)S(1)} all-to-all(bf16[4,64,1,256]{3,1,2,0:T(8,128)(2,1)S(1)} %bitcast.115), channel_id=1, replica_groups=mesh['dp'=4,'seq'=16,'tensor'=8] {'dp'}, dimensions={0} | all-to-all | bytes 262144 | tf_op jit(solution)/shard_map/all_to_all | solution.py:183
  (104 shorter events, 47.7 us)
Async XLA Ops:
  6.5 72.9 %all-gather.2.cloned.1.call-start = ((), (), s32[]{:S(2)}) async-start(), calls=%async_computation.6 | async-start | bytes 2785280 | tf_op jit(solution)/shard_map/all_gather | solution.py:20
  79.5 1.6 slice-start
  81.1 2.3 copy-start.3
  81.1 2.3 copy-start.5
  81.1 2.3 copy-start.6
  125.9 17.9 %all-to-all-start.1 = ((f32[16,1,512]{2,1,0:T(1,128)}), f32[16,1,512]{2,1,0:T(1,128)S(1)}, u32[]{:S(2)}, u32[]{:S(2)}) async-start(f32[16,1,512]{2,1,0:T(1,128)} %reshape.252), calls=%async_computation.1 | async-start | bytes 65536 | tf_op jit(solution)/shard_map/all_to_all | solution.py:125
  157.9 5.0 %copy-start.2 = (bf16[1,64,1024]{2,1,0:T(8,128)(2,1)S(1)}, bf16[1,64,1024]{2,1,0:T(8,128)(2,1)}, u32[]{:S(2)}) copy-start(bf16[1,64,1024]{2,1,0:T(8,128)(2,1)} %param.11) | copy-start | bytes 393220
  157.9 5.1 %copy-start.4 = (s32[1,64]{1,0:T(1,128)S(1)}, s32[1,64]{1,0:T(1,128)}, u32[]{:S(2)}) copy-start(s32[1,64]{1,0:T(1,128)} %param.18) | copy-start | bytes 772
  157.9 5.3 %copy-start = (bf16[1,1024,1280]{2,1,0:T(8,128)(2,1)S(1)}, bf16[1,1024,1280]{2,1,0:T(8,128)(2,1)}, u32[]{:S(2)}) copy-start(bf16[1,1024,1280]{2,1,0:T(8,128)(2,1)} %all-gather.2.cloned.1.call-done) | copy-start | bytes 7864324
  157.9 185.7 %all-to-all-start = ((f32[1,1,1024,8,128]{4,3,1,0,2:T(8,128)}), f32[1,1,1024,8,128]{4,3,1,0,2:T(8,128)}, u32[]{:S(2)}, u32[]{:S(2)}) async-start(f32[1,1,1024,8,128]{4,3,1,0,2:T(8,128)} %bitcast.110), calls=%async_computation | async-start | bytes 8388608 | tf_op jit(solution)/shard_map/all_to_all | solution.py:127
  343.5 3.1 copy-start.1
  348.3 11.0 %all-to-all-start.3 = ((bf16[4,1,64,1024]{3,2,1,0:T(8,128)(2,1)}), bf16[4,1,64,1024]{3,2,1,0:T(8,128)(2,1)S(1)}, u32[]{:S(2)}, u32[]{:S(2)}) async-start(bf16[4,1,64,1024]{3,2,1,0:T(8,128)(2,1)} %broadcast_in_dim.61), calls=%async_computation.3 | async-start | bytes 1048576 | tf_op jit(solution)/shard_map/all_to_all | solution.py:31
Sparse Core Ops, SparseCore 0:
  9.4 70.0 all-gather.1
where the time goes:
time: 416 us; the launch traced here: 414 us
  waiting for transfers between devices  224 us (54%)
  blocking collectives  80.9 us (19%)
  matrix products  32.5 us (8%)
  other arithmetic  24.7 us (6%)
  local copies, waits for them, and re-layouts  21.7 us (5%)
  starting transfers between devices  15.6 us (4%)
  between operations  14.3 us (3%)
    all_to_all x1, waiting for transfers between devices, local(): lax.all_to_all(cache_partial[None], 'seq', split_axis=2, concat_axis=0, t...  170 us
    all_gather x1, waiting for transfers between devices, in_one_piece(): lax.all_gather(both, axis, axis=dim, tiled=True)  44.3 us
    all_to_all x1, blocking collectives, summed_on_arrival(): lax.all_to_all(parts, axis, split_axis=0, concat_axis=0, tiled=True)  35.6 us
    unnamed x1, blocking collectives  23.8 us
    all_to_all x1, blocking collectives, local(): lax.all_to_all(cache_sum[None], 'seq', split_axis=2, concat_axis=0, tiled...  14 us
    dot_general x8, matrix products, softmax_terms(): jnp.dot(weights.astype(jnp.bfloat16), value_rows, preferred_element_type=...  13.5 us
    dot_general x8, matrix products, masked_terms(): jnp.dot(query_rows, key_rows.T, preferred_element_type=jnp.float32)  12.8 us
    all_to_all x1, waiting for transfers between devices, local(): lax.all_to_all(cache_top[None], 'seq', split_axis=2, concat_axis=0, tiled...  9.01 us
  transfers between devices with their start and end apart: 4, of which 4 were waited for; matrix products, arithmetic and copies ran while one was open for 5% of the time, Pallas kernels for 0%

commit v1 on v0

v1 whole, which is shorter than its diff:
```python
import math

import jax
import jax.numpy as jnp
from jax import lax
from jax.experimental import pallas as pl
from jax.experimental.pallas import tpu as pltpu
from jax.sharding import Mesh
from jax.sharding import PartitionSpec as P

HD = 128
masked_score = -1e30
to_log2 = 1.4426950408889634


def contract_last(a, b):
    return lax.dot_general(a, b, (((1,), (1,)), ((), ())), preferred_element_type=jnp.float32)


def dot(a, b):
    return lax.dot_general(a, b, (((1,), (0,)), ((), ())), preferred_element_type=jnp.float32)


def lane_tiles(x):
    return [x[:, i : i + HD] for i in range(0, x.shape[1], HD)]


def attend_kernel(sizes, own, last, *refs):
    slots, fresh, groups, chunks = sizes
    place, q_ref, doc_ref, kv_ref = refs[:4]
    refs = refs[4:]
    if own:
        state = None
        outs = refs
    else:
        state = refs[:3]
        outs = refs[3:]
    my = place[0].astype(jnp.float32)
    code_at = 2 * slots + 2 * fresh
    lanes = lax.broadcasted_iota(jnp.int32, (1, HD), 1)
    row_fresh = None
    origin = None
    for c in range(chunks):
        row = kv_ref[c, pl.ds(code_at, 16), :].astype(jnp.float32)
        mine = row[slots // HD : slots // HD + 1]
        start = row[slots // HD + 1 : slots // HD + 2]
        here = (lanes // fresh) == c
        mine = jnp.where(here, mine, -1.0)
        row_fresh = mine if c == 0 else jnp.where(here, mine, row_fresh)
        origin = start if c == 0 else jnp.where(here, start, origin)
    if not own:
        row_fresh = jnp.where(origin < my, row_fresh, -1.0)
    cache_codes = [
        kv_ref[c, pl.ds(code_at, 16), :].astype(jnp.float32)[i : i + 1]
        for c in range(chunks)
        for i in range(slots // HD)
    ]
    fresh_keys = [kv_ref[c, pl.ds(2 * slots, fresh), :] for c in range(chunks)]
    fresh_values = [kv_ref[c, pl.ds(2 * slots + fresh, fresh), :] for c in range(chunks)]
    if chunks == 1:
        blank = jnp.zeros((HD - fresh, HD), jnp.bfloat16)
        fresh_keys.append(blank)
        fresh_values.append(blank)
    fresh_keys = jnp.concatenate(fresh_keys, axis=0)
    fresh_values = jnp.concatenate(fresh_values, axis=0)
    tokens = doc_ref.shape[0]
    block = groups * tokens
    row_doc = jnp.concatenate([doc_ref[...]] * groups, axis=0)
    scale = to_log2 * HD ** (-0.5)

    def body(b, carry):
        at = pl.multiple_of(b * block, block)
        rows = pl.ds(at, block)
        q = q_ref[rows, :]
        tiles = []
        for c in range(chunks):
            tiles += lane_tiles(contract_last(q, kv_ref[c, pl.ds(0, slots), :]))
        tiles = [
            jnp.where(code == row_doc, t * scale, masked_score)
            for t, code in zip(tiles, cache_codes, strict=True)
        ]
        late = contract_last(q, fresh_keys)
        seen = row_fresh == row_doc
        if own:
            token = lax.broadcasted_iota(jnp.int32, (block, HD), 0) % tokens
            k = lax.broadcasted_iota(jnp.int32, (block, HD), 1)
            seen = seen & (k <= token)
        tiles.append(jnp.where(seen, late * scale, masked_score))
        top = tiles[0]
        for t in tiles[1:]:
            top = jnp.maximum(top, t)
        top = jnp.max(top, axis=1, keepdims=True)
        if state is not None:
            before = state[1][rows, :]
            top = jnp.maximum(before, top)
            fade = jnp.exp2(before - top)
        else:
            top = jnp.broadcast_to(top, (block, HD))
        tiles = [jnp.exp2(t - top) for t in tiles]
        total = tiles[0]
        for t in tiles[1:]:
            total = total + t
        weights = [t.astype(jnp.bfloat16) for t in tiles]
        each = slots // HD
        summed = dot(weights[-1], fresh_values)
        for c in range(chunks):
            part = jnp.concatenate(weights[c * each : (c + 1) * each], axis=1)
            summed = summed + dot(part, kv_ref[c, pl.ds(slots, slots), :])
        if state is not None:
            total = total + state[2][rows, :] * fade
            summed = summed + state[0][rows, :] * fade
        if last:
            value = summed / jnp.sum(total, axis=1, keepdims=True)
            value = value.astype(jnp.bfloat16)
            wide = jnp.concatenate([value[g * tokens : (g + 1) * tokens] for g in range(groups)], axis=1)
            width = groups * HD
            for copy in range(outs[0].shape[0]):
                outs[0][copy, :, pl.ds(pl.multiple_of(b * width, width), width)] = wide
        else:
            outs[0][rows, :] = summed
            outs[1][rows, :] = top
            outs[2][rows, :] = total
        return carry

    lax.fori_loop(0, q_ref.shape[0] // block, body, 0)


def attend(place, q, doc, payload, state, slots, fresh, last, copies):
    chunks = payload.shape[0]
    groups = 4
    rows = q.shape[0]
    tokens = doc.shape[0]
    heads = rows // tokens
    own = state is None
    sizes = (slots, fresh, groups, chunks)

    def kernel(*refs):
        attend_kernel(sizes, own, last, *refs)

    if last:
        out_shape = [jax.ShapeDtypeStruct((copies, tokens, heads * HD), jnp.bfloat16)]
    else:
        out_shape = [jax.ShapeDtypeStruct((rows, HD), jnp.float32)] * 3
    args = (place, q, doc, payload, *(() if own else state))
    specs = [pl.BlockSpec(memory_space=pltpu.SMEM)]
    specs += [pl.BlockSpec(memory_space=pltpu.VMEM)] * (len(args) - 1)
    keys = chunks * (slots + fresh)
    return pl.pallas_call(
        kernel,
        out_shape=out_shape,
        in_specs=specs,
        out_specs=[pl.BlockSpec(memory_space=pltpu.VMEM)] * len(out_shape),
        name="attend_last" if last else ("attend_own" if own else "attend_step"),
        cost_estimate=pl.CostEstimate(
            flops=40 * rows * keys * HD,
            bytes_accessed=payload.size * 2 + 6 * rows * HD * 4,
            transcendentals=rows * keys,
        ),
        compiler_params=pltpu.CompilerParams(vmem_limit_bytes=32 * 1024 * 1024),
    )(*args)


def project_kernel(place, a_ref, own_ref, other_ref, out_ref):
    core = place[1]
    packs, each, width = a_ref.shape[0], a_ref.shape[2], a_ref.shape[3]
    mine = a_ref[:, core].reshape(packs * each, width)
    theirs = a_ref[:, 1 - core].reshape(packs * each, width)
    summed = dot(mine, own_ref[...]) + dot(theirs, other_ref[...])
    out_ref[...] = summed.astype(jnp.bfloat16).reshape(packs, 1, each, summed.shape[1])


def project(place, a, own, other, pieces):
    packs, _, each, width = a.shape
    cols = own.shape[1] // pieces
    return pl.pallas_call(
        project_kernel,
        grid=(pieces,),
        out_shape=jax.ShapeDtypeStruct((packs, pieces, each, cols), jnp.bfloat16),
        in_specs=[
            pl.BlockSpec(memory_space=pltpu.SMEM),
            pl.BlockSpec(a.shape, lambda j: (0, 0, 0, 0)),
            pl.BlockSpec((width, cols), lambda j: (0, j)),
            pl.BlockSpec((width, cols), lambda j: (0, j)),
        ],
        out_specs=pl.BlockSpec((packs, 1, each, cols), lambda j: (0, j, 0, 0)),
        name="project",
        cost_estimate=pl.CostEstimate(
            flops=4 * packs * each * width * own.shape[1],
            bytes_accessed=4 * width * own.shape[1],
            transcendentals=0,
        ),
        compiler_params=pltpu.CompilerParams(vmem_limit_bytes=32 * 1024 * 1024),
    )(place, a, own, other)


def swaps(size):
    plans = []
    for shift in (0, 1):
        pairs = []
        for core in (0, 1):
            for s in range(size):
                odd = (s + core + shift) % 2
                pairs.append((s * 2 + core, ((s + (1 if odd == 0 else -1)) % size) * 2 + core))
        plans.append(pairs)
    return plans


def local(
    queries,
    new_keys,
    new_values,
    cache_keys,
    cache_values,
    keep_lengths,
    cache_doc,
    new_doc,
    out_weight,
):
    ring = lax.axis_size("seq")
    packs, mesh_x, cores = lax.axis_size("dp"), lax.axis_size("x"), lax.axis_size("core")
    my = lax.axis_index("seq")
    core = lax.axis_index("core")
    place = jnp.stack([my, core]).astype(jnp.int32)
    fresh = queries.shape[1]
    heads = queries.shape[2] // HD
    slots = cache_keys.shape[1]
    other_weight = lax.ppermute(out_weight, "core", [(0, 1), (1, 0)])

    visible = jnp.arange(slots, dtype=jnp.int32) < keep_lengths[0, 0]
    cache_code = jnp.where(visible, cache_doc[0], -1).astype(jnp.bfloat16).reshape(slots // HD, HD)
    new_code = jnp.tile(new_doc.astype(jnp.bfloat16), (1, HD // fresh))
    origin = jnp.full((1, HD), my, jnp.int32).astype(jnp.bfloat16)
    spare = jnp.zeros((16 - slots // HD - 2, HD), jnp.bfloat16)
    own = jnp.concatenate(
        [cache_keys[0], cache_values[0], new_keys[0], new_values[0], cache_code, new_code, origin, spare],
        axis=0,
    )[None]
    q = queries[0].reshape(fresh, heads, HD).transpose(1, 0, 2).reshape(heads * fresh, HD)
    doc = jnp.broadcast_to(new_doc[0].astype(jnp.float32)[:, None], (fresh, HD))

    plans = swaps(ring)

    def swap(x, step):
        return lax.ppermute(x, ("seq", "core"), plans[step % 2])

    def step(payload, state, last=False):
        return attend(place, q, doc, payload, state, slots, fresh, last, packs)

    steps = ring // 2
    payload = swap(own, 0)
    state = step(own, None)
    arrived = swap(jnp.concatenate([own, payload], axis=0), 1)
    state = step(payload, state)
    for s in range(2, steps):
        payload, arrived = arrived, swap(arrived, s)
        state = step(payload, state)
    (attended,) = step(arrived, state, last=True)

    each = fresh // cores
    tiles = lax.all_to_all(
        attended.reshape(packs * cores, each, heads * HD), ("dp", "core"), 0, 0, tiled=True
    ).reshape(packs, cores, each, heads * HD)
    pieces = project(place, tiles, out_weight, other_weight, mesh_x * cores)
    width = pieces.shape[3]
    arrived = lax.all_to_all(
        pieces.reshape(packs * mesh_x * cores, each, width), ("dp", "x", "core"), 0, 0, tiled=True
    )
    arrived = arrived.reshape(packs, mesh_x, cores, each, width).astype(jnp.float32)
    result = arrived.sum(axis=1).astype(jnp.bfloat16)
    return result.transpose(1, 2, 0, 3).reshape(1, fresh, packs, width)


def solution(mesh):
    shape = dict(mesh.shape)
    cores = 2
    split = Mesh(
        mesh.devices.reshape(shape["dp"], shape["seq"], shape["tensor"] // cores, cores),
        ("dp", "seq", "x", "core"),
    )
    t = ("x", "core")
    placed = (
        P("dp", "seq", t),
        P("dp", "seq", t),
        P("dp", "seq", t),
        P("dp", "seq", t),
        P("dp", "seq", t),
        P("dp", "seq"),
        P("dp", "seq"),
        P("dp", "seq"),
        P(t, "dp"),
    )
    return jax.shard_map(
        local, mesh=split, in_specs=placed, out_specs=P("dp", "seq", None, t), check_vma=False
    )
```

time: 416 us -> 157 us (0.38)
  waiting for transfers between devices: 224 us -> 47.4 us
  blocking collectives: 80.9 us -> 17.3 us
  starting transfers between devices: 15.6 us -> 54.5 us
  matrix products: 32.5 us -> 0 us
  Pallas kernels: 0 us -> 25.8 us
  other arithmetic: 24.7 us -> 1.64 us
  between operations: 14.3 us -> 0.85 us
  local copies, waits for them, and re-layouts: 21.7 us -> 8.32 us
    all_to_all x3 -> x1, waiting for transfers between devices: 179 us -> 9.35 us  [local(): lax.all_to_all(attended.reshape(packs * cores, each, heads * HD), ('dp',...]
    all_gather x1 -> x0, waiting for transfers between devices: 44.3 us -> none  [in_one_piece(): lax.all_gather(both, axis, axis=dim, tiled=True)]
    ppermute x0 -> x9, starting transfers between devices: none -> 40.7 us  [the longest x8 33.3 us: swap(): return lax.ppermute(x, ('seq', 'core'), plans[step % 2])]
    all_to_all x3 -> x1, blocking collectives: 57.1 us -> 17.3 us  [local(): lax.all_to_all(pieces.reshape(packs * mesh_x * cores, each, width), ('dp'...]
    ppermute x0 -> x9, waiting for transfers between devices: none -> 38.1 us  [the longest x8 38.1 us: swap(): return lax.ppermute(x, ('seq', 'core'), plans[step % 2])]
    dot_general x19 -> x0, matrix products: 32.5 us -> none  [the longest x8 13.5 us: softmax_terms(): jnp.dot(weights.astype(jnp.bfloat16), value_rows, preferred_element_type=...]
    pallas_call x0 -> x10, Pallas kernels: none -> 25.8 us  [the longest x9 19.4 us: attend(): pl.pallas_call(kernel, out_shape=out_shape, in_specs=specs, out_specs=[pl...]
    unnamed x1 -> x0, blocking collectives: 23.8 us -> none
  transfers between devices with their start and end apart: 4 -> 10, of which waited for: 4 -> 9; matrix products, arithmetic and copies ran while one was open for 5% -> 1% of each run, Pallas kernels for 0% -> 12%
where the time goes in v1:
time: 157 us; the launch traced here: 156 us
  starting transfers between devices  54.5 us (35%)
  waiting for transfers between devices  47.4 us (30%)
  Pallas kernels  25.8 us (16%)
  blocking collectives  17.3 us (11%)
  local copies, waits for them, and re-layouts  8.32 us (5%)
  other arithmetic  1.64 us (1%)
    ppermute x8, waiting for transfers between devices, swap(): return lax.ppermute(x, ('seq', 'core'), plans[step % 2])  38.1 us
    ppermute x8, starting transfers between devices, swap(): return lax.ppermute(x, ('seq', 'core'), plans[step % 2])  33.3 us
    pallas_call x9, Pallas kernels, attend(): pl.pallas_call(kernel, out_shape=out_shape, in_specs=specs, out_specs=[pl...  19.4 us
    all_to_all x1, blocking collectives, local(): lax.all_to_all(pieces.reshape(packs * mesh_x * cores, each, width), ('dp'...  17.3 us
    all_to_all x1, starting transfers between devices, local(): lax.all_to_all(attended.reshape(packs * cores, each, heads * HD), ('dp',...  13.7 us
    all_to_all x1, waiting for transfers between devices, local(): lax.all_to_all(attended.reshape(packs * cores, each, heads * HD), ('dp',...  9.35 us
    ppermute x1, starting transfers between devices, local(): other_weight = lax.ppermute(out_weight, 'core', [(0, 1), (1, 0)])  7.46 us
    pallas_call x1, Pallas kernels, project(): pl.pallas_call(project_kernel, grid=(pieces,), out_shape=jax.ShapeDtypeSt...  6.35 us
  transfers between devices with their start and end apart: 10, of which 9 were waited for; matrix products, arithmetic and copies ran while one was open for 1% of the time, Pallas kernels for 12%

profile of v1, /device:TPU:1, one launch (start us, length us, event | category | flops | bytes accessed | tf_op | source)
XLA Modules:
  0.0 155.7 jit_solution(10757017862300234134)
XLA Ops:
  2.2 3.4 %concatenate.6 = bf16[1168,128]{1,0:T(8,128)(2,1)S(1)} concatenate(bf16[512,128]{1,0:T(8,128)(2,1)} %bitcast.45, bf16[512,128]{1,0:T(8,128)(2,1)} %bitcast.46, bf16[64,128]{1,0:T(8,128)(2,1)} %bitcast.47, bf16[64,128]{1,0:T(8,128)(2,1)} %bitcast.48, bf16[4,128]{1,0:T(4,128)(2,1)S(1)} %select_convert_fusion, bf16[1,128]{1,0:T(2,128)(2,1)S(1)} %tile.13, ...), dimensions={0} | concatenate | bytes 598016 | tf_op jit(solution)/shard_map/concatenate | solution.py:234
  5.6 11.9 %collective-permute-start = (bf16[1,1168,128]{2,1,0:T(8,128)(2,1)S(1)}, bf16[1,1168,128]{2,1,0:T(8,128)(2,1)S(1)}, u32[]{:S(2)}, u32[]{:S(2)}) collective-permute-start(bf16[1,1168,128]{2,1,0:T(8,128)(2,1)S(1)} %bitcast.29), channel_id=1, source_target_pairs={{0,8},{8,0},{16,24},{24,16},{32,40},{40,32},{48,56},{56,48},{64,72... | collective-permute-start | bytes 897032 | tf_op jit(solution)/shard_map/ppermute | solution.py:244
  17.6 4.1 %collective-permute-done.refs_3_ = bf16[1,1168,128]{2,1,0:T(8,128)(2,1)S(1)} collective-permute-done((bf16[1,1168,128]{2,1,0:T(8,128)(2,1)S(1)}, bf16[1,1168,128]{2,1,0:T(8,128)(2,1)S(1)}, u32[]{:S(2)}, u32[]{:S(2)}) %collective-permute-start) | collective-permute-done | bytes 299040 | tf_op jit(solution)/shard_map/ppermute | solution.py:244
  23.7 9.1 %collective-permute-done.1.refs_3_ = bf16[2,1168,128]{2,1,0:T(8,128)(2,1)S(1)} collective-permute-done((bf16[2,1168,128]{2,1,0:T(8,128)(2,1)S(1)}, bf16[2,1168,128]{2,1,0:T(8,128)(2,1)S(1)}, u32[]{:S(2)}, u32[]{:S(2)}) %collective-permute-start.1) | collective-permute-done | bytes 598048 | tf_op jit(solution)/shard_map/ppermute | solution.py:244
  32.8 4.6 %collective-permute-start.2 = (bf16[2,1168,128]{2,1,0:T(8,128)(2,1)S(1)}, bf16[2,1168,128]{2,1,0:T(8,128)(2,1)S(1)}, u32[]{:S(2)}, u32[]{:S(2)}) collective-permute-start(bf16[2,1168,128]{2,1,0:T(8,128)(2,1)S(1)} %collective-permute-done.1.refs_3_), channel_id=1, source_target_pairs={{0,8},{8,0},{16,24},{24,16},{32,40},{40,32},{48,56},{56,48},{64,72... | collective-permute-start | bytes 1794056 | tf_op jit(solution)/shard_map/ppermute | solution.py:244
  38.2 6.5 %collective-permute-done.2.refs_3_ = bf16[2,1168,128]{2,1,0:T(8,128)(2,1)S(1)} collective-permute-done((bf16[2,1168,128]{2,1,0:T(8,128)(2,1)S(1)}, bf16[2,1168,128]{2,1,0:T(8,128)(2,1)S(1)}, u32[]{:S(2)}, u32[]{:S(2)}) %collective-permute-start.2) | collective-permute-done | bytes 598048 | tf_op jit(solution)/shard_map/ppermute | solution.py:244
  46.6 7.5 %collective-permute-start.8 = (bf16[1024,2048]{1,0:T(8,128)(2,1)}, bf16[1024,2048]{1,0:T(8,128)(2,1)}, u32[]{:S(2)}, u32[]{:S(2)}) collective-permute-start(bf16[1024,2048]{1,0:T(8,128)(2,1)} %own_ref.1), channel_id=1, source_target_pairs={{0,1},{1,0},{2,3},{3,2},{4,5},{5,4},{6,7},{7,6},{8,9},{9,8},{10,11... | collective-permute-start | bytes 12582920 | tf_op jit(solution)/shard_map/ppermute | solution.py:227
  55.7 4.6 %collective-permute-start.4 = (bf16[2,1168,128]{2,1,0:T(8,128)(2,1)S(1)}, bf16[2,1168,128]{2,1,0:T(8,128)(2,1)S(1)}, u32[]{:S(2)}, u32[]{:S(2)}) collective-permute-start(bf16[2,1168,128]{2,1,0:T(8,128)(2,1)S(1)} %collective-permute-done.3.refs_3_), channel_id=1, source_target_pairs={{0,8},{8,0},{16,24},{24,16},{32,40},{40,32},{48,56},{56,48},{64,72... | collective-permute-start | bytes 1794056 | tf_op jit(solution)/shard_map/ppermute | solution.py:244
  60.3 7.3 %collective-permute-done.4.refs_3_ = bf16[2,1168,128]{2,1,0:T(8,128)(2,1)S(1)} collective-permute-done((bf16[2,1168,128]{2,1,0:T(8,128)(2,1)S(1)}, bf16[2,1168,128]{2,1,0:T(8,128)(2,1)S(1)}, u32[]{:S(2)}, u32[]{:S(2)}) %collective-permute-start.4) | collective-permute-done | bytes 598048 | tf_op jit(solution)/shard_map/ppermute | solution.py:244
  74.1 4.5 %collective-permute-done.5.refs_3_ = bf16[2,1168,128]{2,1,0:T(8,128)(2,1)S(1)} collective-permute-done((bf16[2,1168,128]{2,1,0:T(8,128)(2,1)S(1)}, bf16[2,1168,128]{2,1,0:T(8,128)(2,1)S(1)}, u32[]{:S(2)}, u32[]{:S(2)}) %collective-permute-start.5) | collective-permute-done | bytes 598048 | tf_op jit(solution)/shard_map/ppermute | solution.py:244
  78.6 4.6 %collective-permute-start.6 = (bf16[2,1168,128]{2,1,0:T(8,128)(2,1)S(1)}, bf16[2,1168,128]{2,1,0:T(8,128)(2,1)S(1)}, u32[]{:S(2)}, u32[]{:S(2)}) collective-permute-start(bf16[2,1168,128]{2,1,0:T(8,128)(2,1)S(1)} %collective-permute-done.5.refs_3_), channel_id=1, source_target_pairs={{0,8},{8,0},{16,24},{24,16},{32,40},{40,32},{48,56},{56,48},{64,72... | collective-permute-start | bytes 1794056 | tf_op jit(solution)/shard_map/ppermute | solution.py:244
  83.2 2.1 %attend_step.8 = (f32[512,128]{1,0:T(8,128)S(1)}, f32[512,128]{1,0:T(8,128)S(1)}, f32[512,128]{1,0:T(8,128)S(1)}) custom-call(s32[2]{0:T(128)S(1)} %pad_add_fusion.refs_0_.place, bf16[512,128]{1,0:T(8,128)(2,1)S(1)} %bitcast.34, f32[64,128]{1,0:T(8,128)S(1)} %broadcast_in_dim.19.refs_2_, bf16[2,1168,128]{2,1,0:T(8,128)(2,1)S(1)} %copy-done.2, ...), custom_call_target="tpu_custom_call" | custom-call | flops 3019898880 | bytes 2170880 | tf_op jit(solution)/shard_map/attend_step/pallas_call | solution.py:148
  85.3 2.1 %attend_step.9 = (f32[512,128]{1,0:T(8,128)S(1)}, f32[512,128]{1,0:T(8,128)S(1)}, f32[512,128]{1,0:T(8,128)S(1)}) custom-call(s32[2]{0:T(128)S(1)} %pad_add_fusion.refs_0_.place, bf16[512,128]{1,0:T(8,128)(2,1)S(1)} %bitcast.35, f32[64,128]{1,0:T(8,128)S(1)} %broadcast_in_dim.19.refs_2_, bf16[2,1168,128]{2,1,0:T(8,128)(2,1)S(1)} %collective-permute-done.2.refs_3_, ...), custom_call_target="tpu_custom_call" | custom-call | flops 3019898880 | bytes 2170880 | tf_op jit(solution)/shard_map/attend_step/pallas_call | solution.py:148
  87.4 2.1 %attend_step.10 = (f32[512,128]{1,0:T(8,128)S(1)}, f32[512,128]{1,0:T(8,128)S(1)}, f32[512,128]{1,0:T(8,128)S(1)}) custom-call(s32[2]{0:T(128)S(1)} %pad_add_fusion.refs_0_.place, bf16[512,128]{1,0:T(8,128)(2,1)S(1)} %bitcast.36, f32[64,128]{1,0:T(8,128)S(1)} %broadcast_in_dim.19.refs_2_, bf16[2,1168,128]{2,1,0:T(8,128)(2,1)S(1)} %collective-permute-done.3.refs_3_, ...), custom_call_target="tpu_custom_call" | custom-call | flops 3019898880 | bytes 2170880 | tf_op jit(solution)/shard_map/attend_step/pallas_call | solution.py:148
  92.7 2.1 %attend_step.11 = (f32[512,128]{1,0:T(8,128)S(1)}, f32[512,128]{1,0:T(8,128)S(1)}, f32[512,128]{1,0:T(8,128)S(1)}) custom-call(s32[2]{0:T(128)S(1)} %pad_add_fusion.refs_0_.place, bf16[512,128]{1,0:T(8,128)(2,1)S(1)} %bitcast.37, f32[64,128]{1,0:T(8,128)S(1)} %broadcast_in_dim.19.refs_2_, bf16[2,1168,128]{2,1,0:T(8,128)(2,1)S(1)} %collective-permute-done.4.refs_3_, ...), custom_call_target="tpu_custom_call" | custom-call | flops 3019898880 | bytes 2170880 | tf_op jit(solution)/shard_map/attend_step/pallas_call | solution.py:148
  94.8 2.1 %attend_step.12 = (f32[512,128]{1,0:T(8,128)S(1)}, f32[512,128]{1,0:T(8,128)S(1)}, f32[512,128]{1,0:T(8,128)S(1)}) custom-call(s32[2]{0:T(128)S(1)} %pad_add_fusion.refs_0_.place, bf16[512,128]{1,0:T(8,128)(2,1)S(1)} %bitcast.38, f32[64,128]{1,0:T(8,128)S(1)} %broadcast_in_dim.19.refs_2_, bf16[2,1168,128]{2,1,0:T(8,128)(2,1)S(1)} %collective-permute-done.5.refs_3_, ...), custom_call_target="tpu_custom_call" | custom-call | flops 3019898880 | bytes 2170880 | tf_op jit(solution)/shard_map/attend_step/pallas_call | solution.py:148
  96.9 2.1 %attend_step.13 = (f32[512,128]{1,0:T(8,128)S(1)}, f32[512,128]{1,0:T(8,128)S(1)}, f32[512,128]{1,0:T(8,128)S(1)}) custom-call(s32[2]{0:T(128)S(1)} %pad_add_fusion.refs_0_.place, bf16[512,128]{1,0:T(8,128)(2,1)S(1)} %bitcast.39, f32[64,128]{1,0:T(8,128)S(1)} %broadcast_in_dim.19.refs_2_, bf16[2,1168,128]{2,1,0:T(8,128)(2,1)S(1)} %collective-permute-done.6.refs_3_, ...), custom_call_target="tpu_custom_call" | custom-call | flops 3019898880 | bytes 2170880 | tf_op jit(solution)/shard_map/attend_step/pallas_call | solution.py:148
  99.1 3.7 %collective-permute-done.7.refs_3_ = bf16[2,1168,128]{2,1,0:T(8,128)(2,1)S(1)} collective-permute-done((bf16[2,1168,128]{2,1,0:T(8,128)(2,1)S(1)}, bf16[2,1168,128]{2,1,0:T(8,128)(2,1)S(1)}, u32[]{:S(2)}, u32[]{:S(2)}) %collective-permute-start.7) | collective-permute-done | bytes 598048 | tf_op jit(solution)/shard_map/ppermute | solution.py:244
  102.8 3.2 %attend_last.1 = bf16[4,64,1024]{2,1,0:T(8,128)(2,1)} custom-call(s32[2]{0:T(128)S(1)} %pad_add_fusion.refs_0_.place, bf16[512,128]{1,0:T(8,128)(2,1)S(1)} %bitcast.40, f32[64,128]{1,0:T(8,128)S(1)} %broadcast_in_dim.19.refs_2_, bf16[2,1168,128]{2,1,0:T(8,128)(2,1)S(1)} %collective-permute-done.7.refs_3_, f32[512,128]{1,0:T(8,128)S(1)} %get-tuple-element.50.refs_4_, ...), custom_call_target="tpu_custom_call" | custom-call | flops 3019898880 | bytes 2170880 | tf_op jit(solution)/shard_map/attend_last/pallas_call | solution.py:148
  106.0 13.7 %all-to-all-start = ((bf16[8,32,1024]{2,1,0:T(8,128)(2,1)}), bf16[8,32,1024]{2,1,0:T(8,128)(2,1)S(1)}, u32[]{:S(2)}, u32[]{:S(2)}) async-start(bf16[8,32,1024]{2,1,0:T(8,128)(2,1)} %bitcast.14), calls=%async_computation | async-start | bytes 1048576 | tf_op jit(solution)/shard_map/all_to_all | solution.py:260
  119.7 9.3 %all-to-all-done = bf16[8,32,1024]{2,1,0:T(8,128)(2,1)S(1)} async-done(((bf16[8,32,1024]{2,1,0:T(8,128)(2,1)}), bf16[8,32,1024]{2,1,0:T(8,128)(2,1)S(1)}, u32[]{:S(2)}, u32[]{:S(2)}) %all-to-all-start) | async-done | bytes 524320 | tf_op jit(solution)/shard_map/all_to_all | solution.py:260
  129.1 2.2 %copy-done = bf16[1024,2048]{1,0:T(8,128)(2,1)S(1)} copy-done((bf16[1024,2048]{1,0:T(8,128)(2,1)S(1)}, bf16[1024,2048]{1,0:T(8,128)(2,1)}, u32[]{:S(2)}) %copy-start) | copy-done | bytes 4194328
  131.2 6.3 %project.1 = bf16[4,8,32,256]{3,2,1,0:T(8,128)(2,1)S(1)} custom-call(s32[2]{0:T(128)S(1)} %pad_add_fusion.refs_0_.place, bf16[4,2,32,1024]{3,2,1,0:T(8,128)(2,1)S(1)} %bitcast.27, bf16[1024,2048]{1,0:T(8,128)(2,1)S(1)} %copy-done, bf16[1024,2048]{1,0:T(8,128)(2,1)} %collective-permute-done.8.other_ref), custom_call_target="tpu_custom_call" | custom-call | flops 1073741824 | bytes 8388608 | tf_op jit(solution)/shard_map/project/pallas_call | solution.py:175
  137.6 17.3 %all_to_all.10 = bf16[32,32,256]{2,1,0:T(8,128)(2,1)S(1)} all-to-all(bf16[32,32,256]{2,1,0:T(8,128)(2,1)S(1)} %bitcast.28), channel_id=1, replica_groups=mesh['dp'=4,'seq'=16,'x'=4,'core'=2] {'dp','x','core'}, dimensions={0} | all-to-all | bytes 1048576 | tf_op jit(solution)/shard_map/all_to_all | solution.py:265
  (27 shorter events, 18.2 us)
Async XLA Ops:
  5.6 16.1 %collective-permute-start = (bf16[1,1168,128]{2,1,0:T(8,128)(2,1)S(1)}, bf16[1,1168,128]{2,1,0:T(8,128)(2,1)S(1)}, u32[]{:S(2)}, u32[]{:S(2)}) collective-permute-start(bf16[1,1168,128]{2,1,0:T(8,128)(2,1)S(1)} %bitcast.29), channel_id=1, source_target_pairs={{0,8},{8,0},{16,24},{24,16},{32,40},{40,32},{48,56},{56,48},{64,72... | collective-permute-start | bytes 897032 | tf_op jit(solution)/shard_map/ppermute | solution.py:244
  21.8 11.0 %collective-permute-start.1 = (bf16[2,1168,128]{2,1,0:T(8,128)(2,1)S(1)}, bf16[2,1168,128]{2,1,0:T(8,128)(2,1)S(1)}, u32[]{:S(2)}, u32[]{:S(2)}) collective-permute-start(bf16[2,1168,128]{2,1,0:T(8,128)(2,1)S(1)} %pad_maximum_fusion), channel_id=1, source_target_pairs={{0,120},{8,16},{16,8},{24,32},{32,24},{40,48},{48,40},{56,64},{64,... | collective-permute-start | bytes 1794056 | tf_op jit(solution)/shard_map/ppermute | solution.py:244
  32.8 11.9 %collective-permute-start.2 = (bf16[2,1168,128]{2,1,0:T(8,128)(2,1)S(1)}, bf16[2,1168,128]{2,1,0:T(8,128)(2,1)S(1)}, u32[]{:S(2)}, u32[]{:S(2)}) collective-permute-start(bf16[2,1168,128]{2,1,0:T(8,128)(2,1)S(1)} %collective-permute-done.1.refs_3_), channel_id=1, source_target_pairs={{0,8},{8,0},{16,24},{24,16},{32,40},{40,32},{48,56},{56,48},{64,72... | collective-permute-start | bytes 1794056 | tf_op jit(solution)/shard_map/ppermute | solution.py:244
  37.4 0.8 copy-start.1
  44.7 11.0 %collective-permute-start.3 = (bf16[2,1168,128]{2,1,0:T(8,128)(2,1)S(1)}, bf16[2,1168,128]{2,1,0:T(8,128)(2,1)S(1)}, u32[]{:S(2)}, u32[]{:S(2)}) collective-permute-start(bf16[2,1168,128]{2,1,0:T(8,128)(2,1)S(1)} %collective-permute-done.2.refs_3_), channel_id=1, source_target_pairs={{0,120},{8,16},{16,8},{24,32},{32,24},{40,48},{48,40},{56,64},{64,... | collective-permute-start | bytes 1794056 | tf_op jit(solution)/shard_map/ppermute | solution.py:244
  46.6 73.1 %collective-permute-start.8 = (bf16[1024,2048]{1,0:T(8,128)(2,1)}, bf16[1024,2048]{1,0:T(8,128)(2,1)}, u32[]{:S(2)}, u32[]{:S(2)}) collective-permute-start(bf16[1024,2048]{1,0:T(8,128)(2,1)} %own_ref.1), channel_id=1, source_target_pairs={{0,1},{1,0},{2,3},{3,2},{4,5},{5,4},{6,7},{7,6},{8,9},{9,8},{10,11... | collective-permute-start | bytes 12582920 | tf_op jit(solution)/shard_map/ppermute | solution.py:227
  55.7 11.9 %collective-permute-start.4 = (bf16[2,1168,128]{2,1,0:T(8,128)(2,1)S(1)}, bf16[2,1168,128]{2,1,0:T(8,128)(2,1)S(1)}, u32[]{:S(2)}, u32[]{:S(2)}) collective-permute-start(bf16[2,1168,128]{2,1,0:T(8,128)(2,1)S(1)} %collective-permute-done.3.refs_3_), channel_id=1, source_target_pairs={{0,8},{8,0},{16,24},{24,16},{32,40},{40,32},{48,56},{56,48},{64,72... | collective-permute-start | bytes 1794056 | tf_op jit(solution)/shard_map/ppermute | solution.py:244
  67.6 11.0 %collective-permute-start.5 = (bf16[2,1168,128]{2,1,0:T(8,128)(2,1)S(1)}, bf16[2,1168,128]{2,1,0:T(8,128)(2,1)S(1)}, u32[]{:S(2)}, u32[]{:S(2)}) collective-permute-start(bf16[2,1168,128]{2,1,0:T(8,128)(2,1)S(1)} %collective-permute-done.4.refs_3_), channel_id=1, source_target_pairs={{0,120},{8,16},{16,8},{24,32},{32,24},{40,48},{48,40},{56,64},{64,... | collective-permute-start | bytes 1794056 | tf_op jit(solution)/shard_map/ppermute | solution.py:244
  72.4 10.8 %copy-start.2 = (bf16[2,1168,128]{2,1,0:T(8,128)(2,1)S(1)}, bf16[2,1168,128]{2,1,0:T(8,128)(2,1)}, u32[]{:S(2)}) copy-start(bf16[2,1168,128]{2,1,0:T(8,128)(2,1)} %copy-done.1) | copy-start | bytes 1794052
  78.6 12.1 %collective-permute-start.6 = (bf16[2,1168,128]{2,1,0:T(8,128)(2,1)S(1)}, bf16[2,1168,128]{2,1,0:T(8,128)(2,1)S(1)}, u32[]{:S(2)}, u32[]{:S(2)}) collective-permute-start(bf16[2,1168,128]{2,1,0:T(8,128)(2,1)S(1)} %collective-permute-done.5.refs_3_), channel_id=1, source_target_pairs={{0,8},{8,0},{16,24},{24,16},{32,40},{40,32},{48,56},{56,48},{64,72... | collective-permute-start | bytes 1794056 | tf_op jit(solution)/shard_map/ppermute | solution.py:244
  90.7 12.1 %collective-permute-start.7 = (bf16[2,1168,128]{2,1,0:T(8,128)(2,1)S(1)}, bf16[2,1168,128]{2,1,0:T(8,128)(2,1)S(1)}, u32[]{:S(2)}, u32[]{:S(2)}) collective-permute-start(bf16[2,1168,128]{2,1,0:T(8,128)(2,1)S(1)} %collective-permute-done.6.refs_3_), channel_id=1, source_target_pairs={{0,120},{8,16},{16,8},{24,32},{32,24},{40,48},{48,40},{56,64},{64,... | collective-permute-start | bytes 1794056 | tf_op jit(solution)/shard_map/ppermute | solution.py:244
  106.0 23.1 %all-to-all-start = ((bf16[8,32,1024]{2,1,0:T(8,128)(2,1)}), bf16[8,32,1024]{2,1,0:T(8,128)(2,1)S(1)}, u32[]{:S(2)}, u32[]{:S(2)}) async-start(bf16[8,32,1024]{2,1,0:T(8,128)(2,1)} %bitcast.14), calls=%async_computation | async-start | bytes 1048576 | tf_op jit(solution)/shard_map/all_to_all | solution.py:260
  129.1 2.2 %copy-start = (bf16[1024,2048]{1,0:T(8,128)(2,1)S(1)}, bf16[1024,2048]{1,0:T(8,128)(2,1)}, u32[]{:S(2)}) copy-start(bf16[1024,2048]{1,0:T(8,128)(2,1)} %own_ref.1) | copy-start | bytes 12582916

commit v2 on v1

v2 whole, which is shorter than its diff:
```python
import jax
import jax.numpy as jnp
from jax import lax
from jax.experimental import pallas as pl
from jax.experimental.pallas import tpu as pltpu
from jax.sharding import Mesh
from jax.sharding import PartitionSpec as P


HD = 128
HALVES = 2
CODES = 16
GROUPS = 4
masked_score = -1e30
to_log2 = 1.4426950408889634
VMEM = pl.BlockSpec(memory_space=pltpu.VMEM)
SMEM = pl.BlockSpec(memory_space=pltpu.SMEM)


def contract_last(a, b):
    return lax.dot_general(a, b, (((1,), (1,)), ((), ())), preferred_element_type=jnp.float32)


def dot(a, b):
    return lax.dot_general(a, b, (((1,), (0,)), ((), ())), preferred_element_type=jnp.float32)


def pack_kernel(
    keep_ref, keys, values, new_keys, new_values, doc, new_doc, out_ref, doc_ref, new_doc_ref, sems
):
    slots = keys.shape[0] // HALVES
    fresh = new_keys.shape[0] // HALVES
    copies = [
        pltpu.make_async_copy(doc, doc_ref, sems.at[0]),
        pltpu.make_async_copy(new_doc, new_doc_ref, sems.at[1]),
    ]
    for h in range(HALVES):
        at = 0
        for ref, size in ((keys, slots), (values, slots), (new_keys, fresh), (new_values, fresh)):
            copies.append(
                pltpu.make_async_copy(
                    ref.at[pl.ds(h * size, size)],
                    out_ref.at[h, pl.ds(at, size)],
                    sems.at[len(copies)],
                )
            )
            at += size
    for copy in copies:
        copy.start()
    copies[0].wait()
    copies[1].wait()
    lane = lax.broadcasted_iota(jnp.int32, (1, HD), 1)
    row = lax.broadcasted_iota(jnp.int32, (CODES, HD), 0)
    new_doc = new_doc_ref[...].astype(jnp.float32)
    twice = jnp.concatenate([new_doc] * (HD // new_doc.shape[1]), axis=1)
    turned = pltpu.roll(twice, fresh, 1)
    origin = lax.axis_index("seq").astype(jnp.float32)
    for h in range(HALVES):
        mine = jnp.where((lane // fresh) % HALVES == h, twice, turned)
        codes = jnp.full((CODES, HD), origin, jnp.float32)
        codes = jnp.where(row == slots // HD, mine, codes)
        for i in range(slots // HD):
            first = h * slots + i * HD
            code = doc_ref[:, pl.ds(first, HD)].astype(jnp.float32)
            code = jnp.where(lane + first < keep_ref[0, 0], code, -1.0)
            codes = jnp.where(row == i, code, codes)
        out_ref[h, pl.ds(2 * (slots + fresh), CODES), :] = codes.astype(jnp.bfloat16)
    for copy in copies[2:]:
        copy.wait()


def pack(keep, keys, values, new_keys, new_values, doc, new_doc):
    rows = (keys.shape[0] + values.shape[0] + new_keys.shape[0] + new_values.shape[0]) // HALVES
    return pl.pallas_call(
        pack_kernel,
        out_shape=jax.ShapeDtypeStruct((HALVES, rows + CODES, HD), jnp.bfloat16),
        in_specs=[SMEM] + [pl.BlockSpec(memory_space=pltpu.HBM)] * 6,
        out_specs=VMEM,
        scratch_shapes=[
            pltpu.VMEM(doc.shape, doc.dtype),
            pltpu.VMEM(new_doc.shape, new_doc.dtype),
            pltpu.SemaphoreType.DMA((2 + 4 * HALVES,)),
        ],
        name="pack",
        compiler_params=pltpu.CompilerParams(vmem_limit_bytes=4 * 1024 * 1024),
    )(keep, keys, values, new_keys, new_values, doc, new_doc)


def attend_kernel(own, last, many, *refs):
    queries_ref, doc_ref = refs[:2]
    payloads = refs[2 : 2 + many]
    state = None if own else refs[2 + many : 5 + many]
    outs = refs[2 + many :] if own else refs[5 + many :]
    halves = [(ref, h) for ref in payloads for h in range(ref.shape[0])]
    tokens, width = queries_ref.shape
    fresh = tokens // HALVES
    slots = (payloads[0].shape[1] - CODES - 2 * fresh) // 2
    each = slots // HD
    my = lax.axis_index("seq").astype(jnp.float32)
    lanes = lax.broadcasted_iota(jnp.int32, (1, HD), 1)
    codes = [ref[h, pl.ds(2 * (slots + fresh), CODES), :].astype(jnp.float32) for ref, h in halves]
    cache_codes = [c[i : i + 1] for c in codes for i in range(each)]
    row_fresh = jnp.full((1, HD), -1.0, jnp.float32)
    for n, c in enumerate(codes):
        mine = c[each : each + 1]
        if not own:
            mine = jnp.where(c[each + 1 : each + 2] < my, mine, -1.0)
        row_fresh = jnp.where(lanes // fresh == n, mine, row_fresh)
    new_keys = [ref[h, pl.ds(2 * slots, fresh), :] for ref, h in halves]
    new_values = [ref[h, pl.ds(2 * slots + fresh, fresh), :] for ref, h in halves]
    if len(halves) * fresh < HD:
        blank = jnp.zeros((HD - len(halves) * fresh, HD), jnp.bfloat16)
        new_keys.append(blank)
        new_values.append(blank)
    new_keys = jnp.concatenate(new_keys, axis=0)
    new_values = jnp.concatenate(new_values, axis=0)

    block = GROUPS * tokens
    square = lax.broadcasted_iota(jnp.int32, (tokens, tokens), 0) == lax.broadcasted_iota(
        jnp.int32, (tokens, tokens), 1
    )
    doc = jnp.sum(jnp.where(square, doc_ref[...].astype(jnp.float32), 0.0), axis=1, keepdims=True)
    row_doc = jnp.concatenate([jnp.broadcast_to(doc, (tokens, HD))] * GROUPS, axis=0)
    scale = to_log2 * HD ** (-0.5)

    def body(b, carry):
        rows = pl.ds(pl.multiple_of(b * block, block), block)
        wide = pl.ds(pl.multiple_of(b * GROUPS * HD, GROUPS * HD), GROUPS * HD)
        q = queries_ref[:, wide]
        q = jnp.concatenate([q[:, g * HD : (g + 1) * HD] for g in range(GROUPS)], axis=0)
        tiles = []
        for ref, h in halves:
            scores = contract_last(q, ref[h, pl.ds(0, slots), :])
            tiles += [scores[:, i * HD : (i + 1) * HD] for i in range(each)]
        tiles = [
            jnp.where(code == row_doc, t * scale, masked_score)
            for t, code in zip(tiles, cache_codes, strict=True)
        ]
        late = contract_last(q, new_keys)
        seen = row_fresh == row_doc
        if own:
            token = lax.broadcasted_iota(jnp.int32, (block, HD), 0) % tokens
            seen = seen & (lax.broadcasted_iota(jnp.int32, (block, HD), 1) <= token)
        tiles.append(jnp.where(seen, late * scale, masked_score))
        top = tiles[0]
        for t in tiles[1:]:
            top = jnp.maximum(top, t)
        top = jnp.max(top, axis=1, keepdims=True)
        if own:
            top = jnp.broadcast_to(top, (block, HD))
        else:
            before = state[1][rows, :]
            top = jnp.maximum(before, top)
            fade = jnp.exp2(before - top)
        tiles = [jnp.exp2(t - top) for t in tiles]
        total = tiles[0]
        for t in tiles[1:]:
            total = total + t
        weights = [t.astype(jnp.bfloat16) for t in tiles]
        summed = dot(weights[-1], new_values)
        for n, (ref, h) in enumerate(halves):
            part = jnp.concatenate(weights[n * each : (n + 1) * each], axis=1)
            summed = summed + dot(part, ref[h, pl.ds(slots, slots), :])
        if not own:
            total = total + state[2][rows, :] * fade
            summed = summed + state[0][rows, :] * fade
        if last:
            value = (summed / jnp.sum(total, axis=1, keepdims=True)).astype(jnp.bfloat16)
            value = jnp.concatenate(
                [value[g * tokens : (g + 1) * tokens] for g in range(GROUPS)], axis=1
            )
            for copy in range(outs[0].shape[0]):
                outs[0][copy, :, wide] = value
        else:
            outs[0][rows, :] = summed
            outs[1][rows, :] = top
            outs[2][rows, :] = total
        return carry

    lax.fori_loop(0, width // (GROUPS * HD), body, 0)


def attend(queries, doc, payloads, state, last=0):
    tokens, width = queries.shape
    rows = tokens * width // HD
    own = state is None
    many = len(payloads)

    def kernel(*refs):
        attend_kernel(own, last, many, *refs)

    if last:
        out_shape = [jax.ShapeDtypeStruct((last, tokens, width), jnp.bfloat16)]
    else:
        out_shape = [jax.ShapeDtypeStruct((rows, HD), jnp.float32)] * 3
    args = (queries, doc, *payloads, *(() if own else state))
    keys = sum(p.shape[0] * p.shape[1] for p in payloads) // 2
    return pl.pallas_call(
        kernel,
        out_shape=out_shape,
        in_specs=[VMEM] * len(args),
        out_specs=[VMEM] * len(out_shape),
        name="attend_last" if last else ("attend_own" if own else "attend_step"),
        cost_estimate=pl.CostEstimate(
            flops=16 * rows * keys * HD,
            bytes_accessed=keys * HD * 4 + 6 * rows * HD * 4,
            transcendentals=rows * keys,
        ),
        compiler_params=pltpu.CompilerParams(vmem_limit_bytes=12 * 1024 * 1024),
    )(*args)


def project_kernel(a_ref, own_ref, other_ref, out_ref):
    core = lax.axis_index("core")
    packs, each, width = a_ref.shape[0], a_ref.shape[2], a_ref.shape[3]
    pieces, cols = out_ref.shape[1], out_ref.shape[3]
    mine = a_ref[:, core].reshape(packs * each, width)
    theirs = a_ref[:, 1 - core].reshape(packs * each, width)
    for j in range(pieces):
        at = pl.ds(j * cols, cols)
        summed = dot(mine, own_ref[:, at]) + dot(theirs, other_ref[:, at])
        out_ref[:, j] = summed.astype(jnp.bfloat16).reshape(packs, each, cols)


def project(a, own, other, pieces):
    packs, _, each, width = a.shape
    cols = own.shape[1] // pieces
    block = 2
    return pl.pallas_call(
        project_kernel,
        grid=(pieces // block,),
        out_shape=jax.ShapeDtypeStruct((packs, pieces, each, cols), jnp.bfloat16),
        in_specs=[
            pl.BlockSpec(a.shape, lambda j: (0, 0, 0, 0)),
            pl.BlockSpec((width, cols * block), lambda j: (0, j)),
            pl.BlockSpec((width, cols * block), lambda j: (0, j)),
        ],
        out_specs=pl.BlockSpec((packs, block, each, cols), lambda j: (0, j, 0, 0)),
        name="project",
        cost_estimate=pl.CostEstimate(
            flops=4 * packs * each * width * own.shape[1],
            bytes_accessed=4 * width * own.shape[1],
            transcendentals=0,
        ),
        compiler_params=pltpu.CompilerParams(vmem_limit_bytes=16 * 1024 * 1024),
    )(a, own, other)


def gather_sum_kernel(parts_ref, out_ref):
    packs, terms, cores, each, cols = parts_ref.shape
    for d in range(packs):
        for c in range(cores):
            total = parts_ref[d, 0, c].astype(jnp.float32)
            for t in range(1, terms):
                total = total + parts_ref[d, t, c].astype(jnp.float32)
            out_ref[pl.ds(c * each, each), pl.ds(d * cols, cols)] = total.astype(jnp.bfloat16)


def gather_sum(parts):
    packs, _, cores, each, cols = parts.shape
    return pl.pallas_call(
        gather_sum_kernel,
        out_shape=jax.ShapeDtypeStruct((cores * each, packs * cols), jnp.bfloat16),
        in_specs=[VMEM],
        out_specs=VMEM,
        name="gather_sum",
        compiler_params=pltpu.CompilerParams(vmem_limit_bytes=4 * 1024 * 1024),
    )(parts)


def local(
    queries,
    new_keys,
    new_values,
    cache_keys,
    cache_values,
    keep_lengths,
    cache_doc,
    new_doc,
    out_weight,
):
    ring = lax.axis_size("seq")
    packs, mesh_x, cores = lax.axis_size("dp"), lax.axis_size("x"), lax.axis_size("core")
    fresh = queries.shape[1]
    width = queries.shape[2]

    own = pack(
        keep_lengths, cache_keys[0], cache_values[0], new_keys[0], new_values[0], cache_doc, new_doc
    )
    up = [(i, (i + 1) % ring) for i in range(ring)]
    down = [(i, (i - 1) % ring) for i in range(ring)]

    hops = ring // 2
    state = None
    below = above = own
    for s in range(hops + 1):
        chunks = [below, above] if s else [own]
        if s < hops:
            if s + 1 == hops:
                below, above = below[:1], above[1:]
            below = lax.ppermute(below, "seq", up)
            above = lax.ppermute(above, "seq", down)
            if s == 0:
                other_weight = lax.ppermute(out_weight, "core", [(0, 1), (1, 0)])
            state = attend(queries[0], new_doc, chunks, state)
    (attended,) = attend(queries[0], new_doc, chunks, state, last=packs)

    each = fresh // cores
    tiles = lax.all_to_all(
        attended.reshape(packs * cores, each, width), ("dp", "core"), 0, 0, tiled=True
    ).reshape(packs, cores, each, width)
    pieces = project(tiles, out_weight, other_weight, mesh_x * cores)
    cols = pieces.shape[3]
    arrived = lax.all_to_all(
        pieces.reshape(packs * mesh_x * cores, each, cols), ("dp", "x", "core"), 0, 0, tiled=True
    )
    result = gather_sum(arrived.reshape(packs, mesh_x, cores, each, cols))
    return result.reshape(1, fresh, packs, cols)


def solution(mesh):
    shape = dict(mesh.shape)
    cores = 2
    split = Mesh(
        mesh.devices.reshape(shape["dp"], shape["seq"], shape["tensor"] // cores, cores),
        ("dp", "seq", "x", "core"),
    )
    t = ("x", "core")
    rows = P("dp", "seq", t)
    flat = P("dp", "seq")
    placed = (rows, rows, rows, rows, rows, flat, flat, flat, P(t, "dp"))

    return jax.shard_map(
        local, mesh=split, in_specs=placed, out_specs=P("dp", "seq", None, t), check_vma=False
    )
```

time: 157 us -> 146 us (0.930)
  waiting for transfers between devices: 47.4 us -> 16.7 us
  blocking collectives: 17.3 us -> 38.1 us
  starting transfers between devices: 54.5 us -> 65.5 us
  Pallas kernels: 25.8 us -> 17 us
  other arithmetic: 1.64 us -> 0 us
    ppermute x8 -> x16, starting transfers between devices: 33.3 us -> 56.7 us  [the longest x8 41.4 us: local(): above = lax.ppermute(above, 'seq', down)]
    ppermute x8 -> x16, waiting for transfers between devices: 38.1 us -> 16.7 us  [the longest x8 14.7 us: local(): above = lax.ppermute(above, 'seq', down)]
    all_to_all x1 -> x2, blocking collectives: 17.3 us -> 38.1 us  [the longest x1 20.7 us: local(): lax.all_to_all(attended.reshape(packs * cores, each, width), ('dp', 'core...]
    all_to_all x1 -> x0, starting transfers between devices: 13.7 us -> none  [local(): lax.all_to_all(attended.reshape(packs * cores, each, heads * HD), ('dp',...]
    all_to_all x1 -> x0, waiting for transfers between devices: 9.35 us -> none  [local(): lax.all_to_all(attended.reshape(packs * cores, each, heads * HD), ('dp',...]
    pallas_call x10 -> x12, Pallas kernels: 25.8 us -> 17 us  [the longest x9 13.8 us: attend(): pl.pallas_call(kernel, out_shape=out_shape, in_specs=[VMEM] * len(args),...]
    concatenate x1 -> x0, local copies, waits for them, and re-layouts: 3.44 us -> none  [local(): jnp.concatenate([cache_keys[0], cache_values[0], new_keys[0], new_values[...]
    unnamed x7 -> x18, local copies, waits for them, and re-layouts: 3.93 us -> 6.13 us
  transfers between devices with their start and end apart: 10 -> 17, of which waited for: 9 -> 6; matrix products, arithmetic and copies ran while one was open for 1% -> 0% of each run, Pallas kernels for 12% -> 10%
where the time goes in v2:
time: 146 us; the launch traced here: 145 us
  starting transfers between devices  65.5 us (45%)
  blocking collectives  38.1 us (26%)
  Pallas kernels  17 us (12%)
  waiting for transfers between devices  16.7 us (11%)
  local copies, waits for them, and re-layouts  6.89 us (5%)
    ppermute x8, starting transfers between devices, local(): above = lax.ppermute(above, 'seq', down)  41.4 us
    all_to_all x1, blocking collectives, local(): lax.all_to_all(attended.reshape(packs * cores, each, width), ('dp', 'core...  20.7 us
    all_to_all x1, blocking collectives, local(): lax.all_to_all(pieces.reshape(packs * mesh_x * cores, each, cols), ('dp',...  17.3 us
    ppermute x8, starting transfers between devices, local(): below = lax.ppermute(below, 'seq', up)  15.4 us
    ppermute x8, waiting for transfers between devices, local(): above = lax.ppermute(above, 'seq', down)  14.7 us
    pallas_call x9, Pallas kernels, attend(): pl.pallas_call(kernel, out_shape=out_shape, in_specs=[VMEM] * len(args),...  13.8 us
    ppermute x1, starting transfers between devices, local(): other_weight = lax.ppermute(out_weight, 'core', [(0, 1), (1, 0)])  8.74 us
    unnamed x18, local copies, waits for them, and re-layouts  6.13 us
  transfers between devices with their start and end apart: 17, of which 6 were waited for; matrix products, arithmetic and copies ran while one was open for 0% of the time, Pallas kernels for 10%

profile of v2, /device:TPU:1, one launch (start us, length us, event | category | flops | bytes accessed | tf_op | source)
XLA Modules:
  0.0 145.1 jit_solution(1789849443835352653)
XLA Ops:
  0.0 8.7 %collective-permute-start.16 = (bf16[1024,2048]{1,0:T(8,128)(2,1)}, bf16[1024,2048]{1,0:T(8,128)(2,1)S(1)}, u32[]{:S(2)}, u32[]{:S(2)}) collective-permute-start(bf16[1024,2048]{1,0:T(8,128)(2,1)} %own_ref.1), channel_id=1, source_target_pairs={{0,1},{1,0},{2,3},{3,2},{4,5},{5,4},{6,7},{7,6},{8,9},{9,8},{10,11... | collective-permute-start | bytes 12582920 | tf_op jit(solution)/shard_map/ppermute | solution.py:304
  14.6 5.8 %collective-permute-start.8 = (bf16[2,592,128]{2,1,0:T(8,128)(2,1)S(1)}, bf16[2,592,128]{2,1,0:T(8,128)(2,1)S(1)}, u32[]{:S(2)}, u32[]{:S(2)}) collective-permute-start(bf16[2,592,128]{2,1,0:T(8,128)(2,1)S(1)} %pack.1.refs_2_), channel_id=1, source_target_pairs={{0,120},{8,0},{16,8},{24,16},{32,24},{40,32},{48,40},{56,48},{64,5... | collective-permute-start | bytes 909320 | tf_op jit(solution)/shard_map/ppermute | solution.py:302
  20.4 1.9 %collective-permute-start = (bf16[2,592,128]{2,1,0:T(8,128)(2,1)S(1)}, bf16[2,592,128]{2,1,0:T(8,128)(2,1)S(1)}, u32[]{:S(2)}, u32[]{:S(2)}) collective-permute-start(bf16[2,592,128]{2,1,0:T(8,128)(2,1)S(1)} %pack.1.refs_2_), channel_id=1, source_target_pairs={{0,8},{8,16},{16,24},{24,32},{32,40},{40,48},{48,56},{56,64},{64,7... | collective-permute-start | bytes 909320 | tf_op jit(solution)/shard_map/ppermute | solution.py:301
  22.3 4.6 %collective-permute-done.8.refs_3_ = bf16[2,592,128]{2,1,0:T(8,128)(2,1)S(1)} collective-permute-done((bf16[2,592,128]{2,1,0:T(8,128)(2,1)S(1)}, bf16[2,592,128]{2,1,0:T(8,128)(2,1)S(1)}, u32[]{:S(2)}, u32[]{:S(2)}) %collective-permute-start.8) | collective-permute-done | bytes 303136 | tf_op jit(solution)/shard_map/ppermute | solution.py:302
  26.9 5.3 %collective-permute-start.9 = (bf16[2,592,128]{2,1,0:T(8,128)(2,1)S(1)}, bf16[2,592,128]{2,1,0:T(8,128)(2,1)S(1)}, u32[]{:S(2)}, u32[]{:S(2)}) collective-permute-start(bf16[2,592,128]{2,1,0:T(8,128)(2,1)S(1)} %collective-permute-done.8.refs_3_), channel_id=1, source_target_pairs={{0,120},{8,0},{16,8},{24,16},{32,24},{40,32},{48,40},{56,48},{64,5... | collective-permute-start | bytes 909320 | tf_op jit(solution)/shard_map/ppermute | solution.py:302
  32.2 1.9 %collective-permute-start.1 = (bf16[2,592,128]{2,1,0:T(8,128)(2,1)S(1)}, bf16[2,592,128]{2,1,0:T(8,128)(2,1)S(1)}, u32[]{:S(2)}, u32[]{:S(2)}) collective-permute-start(bf16[2,592,128]{2,1,0:T(8,128)(2,1)S(1)} %collective-permute-done.refs_2_), channel_id=1, source_target_pairs={{0,8},{8,16},{16,24},{24,32},{32,40},{40,48},{48,56},{56,64},{64,7... | collective-permute-start | bytes 909320 | tf_op jit(solution)/shard_map/ppermute | solution.py:301
  34.1 3.7 %collective-permute-done.9.refs_3_ = bf16[2,592,128]{2,1,0:T(8,128)(2,1)S(1)} collective-permute-done((bf16[2,592,128]{2,1,0:T(8,128)(2,1)S(1)}, bf16[2,592,128]{2,1,0:T(8,128)(2,1)S(1)}, u32[]{:S(2)}, u32[]{:S(2)}) %collective-permute-start.9) | collective-permute-done | bytes 303136 | tf_op jit(solution)/shard_map/ppermute | solution.py:302
  37.8 5.3 %collective-permute-start.10 = (bf16[2,592,128]{2,1,0:T(8,128)(2,1)S(1)}, bf16[2,592,128]{2,1,0:T(8,128)(2,1)S(1)}, u32[]{:S(2)}, u32[]{:S(2)}) collective-permute-start(bf16[2,592,128]{2,1,0:T(8,128)(2,1)S(1)} %collective-permute-done.9.refs_3_), channel_id=1, source_target_pairs={{0,120},{8,0},{16,8},{24,16},{32,24},{40,32},{48,40},{56,48},{64,5... | collective-permute-start | bytes 909320 | tf_op jit(solution)/shard_map/ppermute | solution.py:302
  43.2 1.9 %collective-permute-start.2 = (bf16[2,592,128]{2,1,0:T(8,128)(2,1)S(1)}, bf16[2,592,128]{2,1,0:T(8,128)(2,1)S(1)}, u32[]{:S(2)}, u32[]{:S(2)}) collective-permute-start(bf16[2,592,128]{2,1,0:T(8,128)(2,1)S(1)} %collective-permute-done.1.refs_2_), channel_id=1, source_target_pairs={{0,8},{8,16},{16,24},{24,32},{32,40},{40,48},{48,56},{56,64},{64,7... | collective-permute-start | bytes 909320 | tf_op jit(solution)/shard_map/ppermute | solution.py:301
  45.1 2.9 %collective-permute-done.10.refs_3_ = bf16[2,592,128]{2,1,0:T(8,128)(2,1)S(1)} collective-permute-done((bf16[2,592,128]{2,1,0:T(8,128)(2,1)S(1)}, bf16[2,592,128]{2,1,0:T(8,128)(2,1)S(1)}, u32[]{:S(2)}, u32[]{:S(2)}) %collective-permute-start.10) | collective-permute-done | bytes 303136 | tf_op jit(solution)/shard_map/ppermute | solution.py:302
  48.0 5.3 %collective-permute-start.11 = (bf16[2,592,128]{2,1,0:T(8,128)(2,1)S(1)}, bf16[2,592,128]{2,1,0:T(8,128)(2,1)S(1)}, u32[]{:S(2)}, u32[]{:S(2)}) collective-permute-start(bf16[2,592,128]{2,1,0:T(8,128)(2,1)S(1)} %collective-permute-done.10.refs_3_), channel_id=1, source_target_pairs={{0,120},{8,0},{16,8},{24,16},{32,24},{40,32},{48,40},{56,48},{64,5... | collective-permute-start | bytes 909320 | tf_op jit(solution)/shard_map/ppermute | solution.py:302
  53.3 1.9 %collective-permute-start.3 = (bf16[2,592,128]{2,1,0:T(8,128)(2,1)S(1)}, bf16[2,592,128]{2,1,0:T(8,128)(2,1)S(1)}, u32[]{:S(2)}, u32[]{:S(2)}) collective-permute-start(bf16[2,592,128]{2,1,0:T(8,128)(2,1)S(1)} %collective-permute-done.2.refs_2_), channel_id=1, source_target_pairs={{0,8},{8,16},{16,24},{24,32},{32,40},{40,48},{48,56},{56,64},{64,7... | collective-permute-start | bytes 909320 | tf_op jit(solution)/shard_map/ppermute | solution.py:301
  57.0 5.5 %collective-permute-start.12 = (bf16[2,592,128]{2,1,0:T(8,128)(2,1)S(1)}, bf16[2,592,128]{2,1,0:T(8,128)(2,1)S(1)}, u32[]{:S(2)}, u32[]{:S(2)}) collective-permute-start(bf16[2,592,128]{2,1,0:T(8,128)(2,1)S(1)} %collective-permute-done.11.refs_3_), channel_id=1, source_target_pairs={{0,120},{8,0},{16,8},{24,16},{32,24},{40,32},{48,40},{56,48},{64,5... | collective-permute-start | bytes 909320 | tf_op jit(solution)/shard_map/ppermute | solution.py:302
  62.5 1.9 %collective-permute-start.4 = (bf16[2,592,128]{2,1,0:T(8,128)(2,1)S(1)}, bf16[2,592,128]{2,1,0:T(8,128)(2,1)S(1)}, u32[]{:S(2)}, u32[]{:S(2)}) collective-permute-start(bf16[2,592,128]{2,1,0:T(8,128)(2,1)S(1)} %collective-permute-done.3.refs_2_), channel_id=1, source_target_pairs={{0,8},{8,16},{16,24},{24,32},{32,40},{40,48},{48,56},{56,64},{64,7... | collective-permute-start | bytes 909320 | tf_op jit(solution)/shard_map/ppermute | solution.py:301
  66.3 5.0 %collective-permute-start.13 = (bf16[2,592,128]{2,1,0:T(8,128)(2,1)S(1)}, bf16[2,592,128]{2,1,0:T(8,128)(2,1)S(1)}, u32[]{:S(2)}, u32[]{:S(2)}) collective-permute-start(bf16[2,592,128]{2,1,0:T(8,128)(2,1)S(1)} %collective-permute-done.12.refs_3_), channel_id=1, source_target_pairs={{0,120},{8,0},{16,8},{24,16},{32,24},{40,32},{48,40},{56,48},{64,5... | collective-permute-start | bytes 909320 | tf_op jit(solution)/shard_map/ppermute | solution.py:302
  71.3 1.9 %collective-permute-start.5 = (bf16[2,592,128]{2,1,0:T(8,128)(2,1)S(1)}, bf16[2,592,128]{2,1,0:T(8,128)(2,1)S(1)}, u32[]{:S(2)}, u32[]{:S(2)}) collective-permute-start(bf16[2,592,128]{2,1,0:T(8,128)(2,1)S(1)} %collective-permute-done.4.refs_2_), channel_id=1, source_target_pairs={{0,8},{8,16},{16,24},{24,32},{32,40},{40,48},{48,56},{56,64},{64,7... | collective-permute-start | bytes 909320 | tf_op jit(solution)/shard_map/ppermute | solution.py:301
  79.3 4.6 %collective-permute-start.14 = (bf16[2,592,128]{2,1,0:T(8,128)(2,1)S(1)}, bf16[2,592,128]{2,1,0:T(8,128)(2,1)S(1)}, u32[]{:S(2)}, u32[]{:S(2)}) collective-permute-start(bf16[2,592,128]{2,1,0:T(8,128)(2,1)S(1)} %collective-permute-done.13.refs_3_), channel_id=1, source_target_pairs={{0,120},{8,0},{16,8},{24,16},{32,24},{40,32},{48,40},{56,48},{64,5... | collective-permute-start | bytes 909320 | tf_op jit(solution)/shard_map/ppermute | solution.py:302
  83.9 1.9 %collective-permute-start.6 = (bf16[2,592,128]{2,1,0:T(8,128)(2,1)S(1)}, bf16[2,592,128]{2,1,0:T(8,128)(2,1)S(1)}, u32[]{:S(2)}, u32[]{:S(2)}) collective-permute-start(bf16[2,592,128]{2,1,0:T(8,128)(2,1)S(1)} %collective-permute-done.5.refs_2_), channel_id=1, source_target_pairs={{0,8},{8,16},{16,24},{24,32},{32,40},{40,48},{48,56},{56,64},{64,7... | collective-permute-start | bytes 909320 | tf_op jit(solution)/shard_map/ppermute | solution.py:301
  90.7 4.6 %collective-permute-start.15 = (bf16[1,592,128]{2,1,0:T(8,128)(2,1)S(1)}, bf16[1,592,128]{2,1,0:T(8,128)(2,1)S(1)}, u32[]{:S(2)}, u32[]{:S(2)}) collective-permute-start(bf16[1,592,128]{2,1,0:T(8,128)(2,1)S(1)} %slice.9), channel_id=1, source_target_pairs={{0,120},{8,0},{16,8},{24,16},{32,24},{40,32},{48,40},{56,48},{64,5... | collective-permute-start | bytes 454664 | tf_op jit(solution)/shard_map/ppermute | solution.py:302
  95.3 1.9 %collective-permute-start.7 = (bf16[1,592,128]{2,1,0:T(8,128)(2,1)S(1)}, bf16[1,592,128]{2,1,0:T(8,128)(2,1)S(1)}, u32[]{:S(2)}, u32[]{:S(2)}) collective-permute-start(bf16[1,592,128]{2,1,0:T(8,128)(2,1)S(1)} %slice.8), channel_id=1, source_target_pairs={{0,8},{8,16},{16,24},{24,32},{32,40},{40,48},{48,56},{56,64},{64,7... | collective-permute-start | bytes 454664 | tf_op jit(solution)/shard_map/ppermute | solution.py:301
  100.5 2.0 %collective-permute-done.7.refs_2_ = bf16[1,592,128]{2,1,0:T(8,128)(2,1)S(1)} collective-permute-done((bf16[1,592,128]{2,1,0:T(8,128)(2,1)S(1)}, bf16[1,592,128]{2,1,0:T(8,128)(2,1)S(1)}, u32[]{:S(2)}, u32[]{:S(2)}) %collective-permute-start.7) | collective-permute-done | bytes 151584 | tf_op jit(solution)/shard_map/ppermute | solution.py:301
  103.7 20.7 %all_to_all.10 = bf16[8,32,1024]{2,1,0:T(8,128)(2,1)S(1)} all-to-all(bf16[8,32,1024]{2,1,0:T(8,128)(2,1)S(1)} %bitcast.12), channel_id=1, replica_groups=mesh['dp'=4,'seq'=16,'x'=4,'core'=2] {'dp','core'}, dimensions={0} | all-to-all | bytes 1048576 | tf_op jit(solution)/shard_map/all_to_all | solution.py:309
  124.4 2.6 %project.1 = bf16[4,8,32,256]{3,2,1,0:T(8,128)(2,1)S(1)} custom-call(bf16[4,2,32,1024]{3,2,1,0:T(8,128)(2,1)S(1)} %bitcast.9, bf16[1024,2048]{1,0:T(8,128)(2,1)S(1)} %copy-done, bf16[1024,2048]{1,0:T(8,128)(2,1)S(1)} %collective-permute-done.16.other_ref), custom_call_target="tpu_custom_call" | custom-call | flops 1073741824 | bytes 8388608 | tf_op jit(solution)/shard_map/project/pallas_call | solution.py:229
  127.0 17.3 %all_to_all.11 = bf16[32,32,256]{2,1,0:T(8,128)(2,1)S(1)} all-to-all(bf16[32,32,256]{2,1,0:T(8,128)(2,1)S(1)} %bitcast.10), channel_id=1, replica_groups=mesh['dp'=4,'seq'=16,'x'=4,'core'=2] {'dp','x','core'}, dimensions={0} | all-to-all | bytes 1048576 | tf_op jit(solution)/shard_map/all_to_all | solution.py:314
  (45 shorter events, 25.0 us)
Async XLA Ops:
  0.0 124.4 %collective-permute-start.16 = (bf16[1024,2048]{1,0:T(8,128)(2,1)}, bf16[1024,2048]{1,0:T(8,128)(2,1)S(1)}, u32[]{:S(2)}, u32[]{:S(2)}) collective-permute-start(bf16[1024,2048]{1,0:T(8,128)(2,1)} %own_ref.1), channel_id=1, source_target_pairs={{0,1},{1,0},{2,3},{3,2},{4,5},{5,4},{6,7},{7,6},{8,9},{9,8},{10,11... | collective-permute-start | bytes 12582920 | tf_op jit(solution)/shard_map/ppermute | solution.py:304
  9.4 0.9 copy-start.1
  10.3 0.9 copy-start.2
  11.2 0.7 copy-start.3
  11.9 0.7 copy-start.4
  12.6 0.7 copy-start.5
  14.6 12.3 %collective-permute-start.8 = (bf16[2,592,128]{2,1,0:T(8,128)(2,1)S(1)}, bf16[2,592,128]{2,1,0:T(8,128)(2,1)S(1)}, u32[]{:S(2)}, u32[]{:S(2)}) collective-permute-start(bf16[2,592,128]{2,1,0:T(8,128)(2,1)S(1)} %pack.1.refs_2_), channel_id=1, source_target_pairs={{0,120},{8,0},{16,8},{24,16},{32,24},{40,32},{48,40},{56,48},{64,5... | collective-permute-start | bytes 909320 | tf_op jit(solution)/shard_map/ppermute | solution.py:302
  20.4 11.8 %collective-permute-start = (bf16[2,592,128]{2,1,0:T(8,128)(2,1)S(1)}, bf16[2,592,128]{2,1,0:T(8,128)(2,1)S(1)}, u32[]{:S(2)}, u32[]{:S(2)}) collective-permute-start(bf16[2,592,128]{2,1,0:T(8,128)(2,1)S(1)} %pack.1.refs_2_), channel_id=1, source_target_pairs={{0,8},{8,16},{16,24},{24,32},{32,40},{40,48},{48,56},{56,64},{64,7... | collective-permute-start | bytes 909320 | tf_op jit(solution)/shard_map/ppermute | solution.py:301
  26.9 11.0 %collective-permute-start.9 = (bf16[2,592,128]{2,1,0:T(8,128)(2,1)S(1)}, bf16[2,592,128]{2,1,0:T(8,128)(2,1)S(1)}, u32[]{:S(2)}, u32[]{:S(2)}) collective-permute-start(bf16[2,592,128]{2,1,0:T(8,128)(2,1)S(1)} %collective-permute-done.8.refs_3_), channel_id=1, source_target_pairs={{0,120},{8,0},{16,8},{24,16},{32,24},{40,32},{48,40},{56,48},{64,5... | collective-permute-start | bytes 909320 | tf_op jit(solution)/shard_map/ppermute | solution.py:302
  32.2 11.0 %collective-permute-start.1 = (bf16[2,592,128]{2,1,0:T(8,128)(2,1)S(1)}, bf16[2,592,128]{2,1,0:T(8,128)(2,1)S(1)}, u32[]{:S(2)}, u32[]{:S(2)}) collective-permute-start(bf16[2,592,128]{2,1,0:T(8,128)(2,1)S(1)} %collective-permute-done.refs_2_), channel_id=1, source_target_pairs={{0,8},{8,16},{16,24},{24,32},{32,40},{40,48},{48,56},{56,64},{64,7... | collective-permute-start | bytes 909320 | tf_op jit(solution)/shard_map/ppermute | solution.py:301
  37.8 10.1 %collective-permute-start.10 = (bf16[2,592,128]{2,1,0:T(8,128)(2,1)S(1)}, bf16[2,592,128]{2,1,0:T(8,128)(2,1)S(1)}, u32[]{:S(2)}, u32[]{:S(2)}) collective-permute-start(bf16[2,592,128]{2,1,0:T(8,128)(2,1)S(1)} %collective-permute-done.9.refs_3_), channel_id=1, source_target_pairs={{0,120},{8,0},{16,8},{24,16},{32,24},{40,32},{48,40},{56,48},{64,5... | collective-permute-start | bytes 909320 | tf_op jit(solution)/shard_map/ppermute | solution.py:302
  43.2 10.1 %collective-permute-start.2 = (bf16[2,592,128]{2,1,0:T(8,128)(2,1)S(1)}, bf16[2,592,128]{2,1,0:T(8,128)(2,1)S(1)}, u32[]{:S(2)}, u32[]{:S(2)}) collective-permute-start(bf16[2,592,128]{2,1,0:T(8,128)(2,1)S(1)} %collective-permute-done.1.refs_2_), channel_id=1, source_target_pairs={{0,8},{8,16},{16,24},{24,32},{32,40},{40,48},{48,56},{56,64},{64,7... | collective-permute-start | bytes 909320 | tf_op jit(solution)/shard_map/ppermute | solution.py:301
  48.0 9.0 %collective-permute-start.11 = (bf16[2,592,128]{2,1,0:T(8,128)(2,1)S(1)}, bf16[2,592,128]{2,1,0:T(8,128)(2,1)S(1)}, u32[]{:S(2)}, u32[]{:S(2)}) collective-permute-start(bf16[2,592,128]{2,1,0:T(8,128)(2,1)S(1)} %collective-permute-done.10.refs_3_), channel_id=1, source_target_pairs={{0,120},{8,0},{16,8},{24,16},{32,24},{40,32},{48,40},{56,48},{64,5... | collective-permute-start | bytes 909320 | tf_op jit(solution)/shard_map/ppermute | solution.py:302
  53.3 9.2 %collective-permute-start.3 = (bf16[2,592,128]{2,1,0:T(8,128)(2,1)S(1)}, bf16[2,592,128]{2,1,0:T(8,128)(2,1)S(1)}, u32[]{:S(2)}, u32[]{:S(2)}) collective-permute-start(bf16[2,592,128]{2,1,0:T(8,128)(2,1)S(1)} %collective-permute-done.2.refs_2_), channel_id=1, source_target_pairs={{0,8},{8,16},{16,24},{24,32},{32,40},{40,48},{48,56},{56,64},{64,7... | collective-permute-start | bytes 909320 | tf_op jit(solution)/shard_map/ppermute | solution.py:301
  57.0 9.3 %collective-permute-start.12 = (bf16[2,592,128]{2,1,0:T(8,128)(2,1)S(1)}, bf16[2,592,128]{2,1,0:T(8,128)(2,1)S(1)}, u32[]{:S(2)}, u32[]{:S(2)}) collective-permute-start(bf16[2,592,128]{2,1,0:T(8,128)(2,1)S(1)} %collective-permute-done.11.refs_3_), channel_id=1, source_target_pairs={{0,120},{8,0},{16,8},{24,16},{32,24},{40,32},{48,40},{56,48},{64,5... | collective-permute-start | bytes 909320 | tf_op jit(solution)/shard_map/ppermute | solution.py:302
  62.5 8.8 %collective-permute-start.4 = (bf16[2,592,128]{2,1,0:T(8,128)(2,1)S(1)}, bf16[2,592,128]{2,1,0:T(8,128)(2,1)S(1)}, u32[]{:S(2)}, u32[]{:S(2)}) collective-permute-start(bf16[2,592,128]{2,1,0:T(8,128)(2,1)S(1)} %collective-permute-done.3.refs_2_), channel_id=1, source_target_pairs={{0,8},{8,16},{16,24},{24,32},{32,40},{40,48},{48,56},{56,64},{64,7... | collective-permute-start | bytes 909320 | tf_op jit(solution)/shard_map/ppermute | solution.py:301
  66.3 13.0 %collective-permute-start.13 = (bf16[2,592,128]{2,1,0:T(8,128)(2,1)S(1)}, bf16[2,592,128]{2,1,0:T(8,128)(2,1)S(1)}, u32[]{:S(2)}, u32[]{:S(2)}) collective-permute-start(bf16[2,592,128]{2,1,0:T(8,128)(2,1)S(1)} %collective-permute-done.12.refs_3_), channel_id=1, source_target_pairs={{0,120},{8,0},{16,8},{24,16},{32,24},{40,32},{48,40},{56,48},{64,5... | collective-permute-start | bytes 909320 | tf_op jit(solution)/shard_map/ppermute | solution.py:302
  71.3 12.6 %collective-permute-start.5 = (bf16[2,592,128]{2,1,0:T(8,128)(2,1)S(1)}, bf16[2,592,128]{2,1,0:T(8,128)(2,1)S(1)}, u32[]{:S(2)}, u32[]{:S(2)}) collective-permute-start(bf16[2,592,128]{2,1,0:T(8,128)(2,1)S(1)} %collective-permute-done.4.refs_2_), channel_id=1, source_target_pairs={{0,8},{8,16},{16,24},{24,32},{32,40},{40,48},{48,56},{56,64},{64,7... | collective-permute-start | bytes 909320 | tf_op jit(solution)/shard_map/ppermute | solution.py:301
  73.9 0.9 copy-start.8
  79.3 11.4 %collective-permute-start.14 = (bf16[2,592,128]{2,1,0:T(8,128)(2,1)S(1)}, bf16[2,592,128]{2,1,0:T(8,128)(2,1)S(1)}, u32[]{:S(2)}, u32[]{:S(2)}) collective-permute-start(bf16[2,592,128]{2,1,0:T(8,128)(2,1)S(1)} %collective-permute-done.13.refs_3_), channel_id=1, source_target_pairs={{0,120},{8,0},{16,8},{24,16},{32,24},{40,32},{48,40},{56,48},{64,5... | collective-permute-start | bytes 909320 | tf_op jit(solution)/shard_map/ppermute | solution.py:302
  83.9 11.4 %collective-permute-start.6 = (bf16[2,592,128]{2,1,0:T(8,128)(2,1)S(1)}, bf16[2,592,128]{2,1,0:T(8,128)(2,1)S(1)}, u32[]{:S(2)}, u32[]{:S(2)}) collective-permute-start(bf16[2,592,128]{2,1,0:T(8,128)(2,1)S(1)} %collective-permute-done.5.refs_2_), channel_id=1, source_target_pairs={{0,8},{8,16},{16,24},{24,32},{32,40},{40,48},{48,56},{56,64},{64,7... | collective-permute-start | bytes 909320 | tf_op jit(solution)/shard_map/ppermute | solution.py:301
  90.7 9.8 %collective-permute-start.15 = (bf16[1,592,128]{2,1,0:T(8,128)(2,1)S(1)}, bf16[1,592,128]{2,1,0:T(8,128)(2,1)S(1)}, u32[]{:S(2)}, u32[]{:S(2)}) collective-permute-start(bf16[1,592,128]{2,1,0:T(8,128)(2,1)S(1)} %slice.9), channel_id=1, source_target_pairs={{0,120},{8,0},{16,8},{24,16},{32,24},{40,32},{48,40},{56,48},{64,5... | collective-permute-start | bytes 454664 | tf_op jit(solution)/shard_map/ppermute | solution.py:302
  95.3 7.1 %collective-permute-start.7 = (bf16[1,592,128]{2,1,0:T(8,128)(2,1)S(1)}, bf16[1,592,128]{2,1,0:T(8,128)(2,1)S(1)}, u32[]{:S(2)}, u32[]{:S(2)}) collective-permute-start(bf16[1,592,128]{2,1,0:T(8,128)(2,1)S(1)} %slice.8), channel_id=1, source_target_pairs={{0,8},{8,16},{16,24},{24,32},{32,40},{40,48},{48,56},{56,64},{64,7... | collective-permute-start | bytes 454664 | tf_op jit(solution)/shard_map/ppermute | solution.py:301
  98.8 25.6 %copy-start = (bf16[1024,2048]{1,0:T(8,128)(2,1)S(1)}, bf16[1024,2048]{1,0:T(8,128)(2,1)}, u32[]{:S(2)}) copy-start(bf16[1024,2048]{1,0:T(8,128)(2,1)} %own_ref.1) | copy-start | bytes 12582916
  (2 other events, 1.3 us)

commit v3 on v2

--- a/solution.py
+++ b/solution.py
@@ -26,8 +26,21 @@
 
 
 def pack_kernel(
-    keep_ref, keys, values, new_keys, new_values, doc, new_doc, out_ref, doc_ref, new_doc_ref, sems
+    keep_ref,
+    queries,
+    keys,
+    values,
+    new_keys,
+    new_values,
+    doc,
+    new_doc,
+    out_ref,
+    ask_ref,
+    doc_ref,
+    new_doc_ref,
+    sems,
 ):
+    tokens, width = queries.shape
     slots = keys.shape[0] // HALVES
     fresh = new_keys.shape[0] // HALVES
     copies = [
@@ -45,6 +58,9 @@
                 )
             )
             at += size
+    copies.append(
+        pltpu.make_async_copy(queries, ask_ref.at[pl.ds(0, tokens)], sems.at[len(copies)])
+    )
     for copy in copies:
         copy.start()
     copies[0].wait()
@@ -65,47 +81,55 @@
             code = jnp.where(lane + first < keep_ref[0, 0], code, -1.0)
             codes = jnp.where(row == i, code, codes)
         out_ref[h, pl.ds(2 * (slots + fresh), CODES), :] = codes.astype(jnp.bfloat16)
+    asked = jnp.concatenate([twice, jnp.zeros((1, width - HD), jnp.float32)], axis=1)
+    asked = jnp.broadcast_to(asked, (CODES, width))
+    ask_ref[pl.ds(tokens, CODES), :] = asked.astype(jnp.bfloat16)
     for copy in copies[2:]:
         copy.wait()
 
 
-def pack(keep, keys, values, new_keys, new_values, doc, new_doc):
+def pack(keep, queries, keys, values, new_keys, new_values, doc, new_doc):
     rows = (keys.shape[0] + values.shape[0] + new_keys.shape[0] + new_values.shape[0]) // HALVES
     return pl.pallas_call(
         pack_kernel,
-        out_shape=jax.ShapeDtypeStruct((HALVES, rows + CODES, HD), jnp.bfloat16),
-        in_specs=[SMEM] + [pl.BlockSpec(memory_space=pltpu.HBM)] * 6,
-        out_specs=VMEM,
+        out_shape=[
+            jax.ShapeDtypeStruct((HALVES, rows + CODES, HD), jnp.bfloat16),
+            jax.ShapeDtypeStruct((queries.shape[0] + CODES, queries.shape[1]), jnp.bfloat16),
+        ],
+        in_specs=[SMEM] + [pl.BlockSpec(memory_space=pl.ANY)] * 7,
+        out_specs=[VMEM] * 2,
         scratch_shapes=[
             pltpu.VMEM(doc.shape, doc.dtype),
             pltpu.VMEM(new_doc.shape, new_doc.dtype),
-            pltpu.SemaphoreType.DMA((2 + 4 * HALVES,)),
+            pltpu.SemaphoreType.DMA((3 + 4 * HALVES,)),
         ],
         name="pack",
-        compiler_params=pltpu.CompilerParams(vmem_limit_bytes=4 * 1024 * 1024),
-    )(keep, keys, values, new_keys, new_values, doc, new_doc)
-
-
-def attend_kernel(own, last, many, *refs):
-    queries_ref, doc_ref = refs[:2]
-    payloads = refs[2 : 2 + many]
-    state = None if own else refs[2 + many : 5 + many]
-    outs = refs[2 + many :] if own else refs[5 + many :]
+        compiler_params=pltpu.CompilerParams(vmem_limit_bytes=60 * 1024 * 1024),
+    )(keep, queries, keys, values, new_keys, new_values, doc, new_doc)
+
+
+def attend_kernel(first, mine, last, many, *refs):
+    ask_ref = refs[0]
+    payloads = refs[1 : 1 + many]
+    state = None if first else refs[1 + many : 4 + many]
+    outs = refs[1 + many :] if first else refs[4 + many :]
     halves = [(ref, h) for ref in payloads for h in range(ref.shape[0])]
-    tokens, width = queries_ref.shape
+    tokens, width = ask_ref.shape
+    tokens = tokens - CODES
     fresh = tokens // HALVES
     slots = (payloads[0].shape[1] - CODES - 2 * fresh) // 2
     each = slots // HD
-    my = lax.axis_index("seq").astype(jnp.float32)
+    seq = lax.axis_index("seq")
+    place = (seq if mine else seq + 1 - 2 * lax.rem(seq, 2)).astype(jnp.float32)
     lanes = lax.broadcasted_iota(jnp.int32, (1, HD), 1)
     codes = [ref[h, pl.ds(2 * (slots + fresh), CODES), :].astype(jnp.float32) for ref, h in halves]
     cache_codes = [c[i : i + 1] for c in codes for i in range(each)]
     row_fresh = jnp.full((1, HD), -1.0, jnp.float32)
     for n, c in enumerate(codes):
-        mine = c[each : each + 1]
-        if not own:
-            mine = jnp.where(c[each + 1 : each + 2] < my, mine, -1.0)
-        row_fresh = jnp.where(lanes // fresh == n, mine, row_fresh)
+        seen = c[each : each + 1]
+        if not (first and mine):
+            seen = jnp.where(c[each + 1 : each + 2] < place, seen, -1.0)
+        row_fresh = jnp.where(lanes // fresh == n, seen, row_fresh)
     new_keys = [ref[h, pl.ds(2 * slots, fresh), :] for ref, h in halves]
     new_values = [ref[h, pl.ds(2 * slots + fresh, fresh), :] for ref, h in halves]
     if len(halves) * fresh < HD:
@@ -116,17 +140,18 @@
     new_values = jnp.concatenate(new_values, axis=0)
 
     block = GROUPS * tokens
-    square = lax.broadcasted_iota(jnp.int32, (tokens, tokens), 0) == lax.broadcasted_iota(
-        jnp.int32, (tokens, tokens), 1
-    )
-    doc = jnp.sum(jnp.where(square, doc_ref[...].astype(jnp.float32), 0.0), axis=1, keepdims=True)
+    square = lax.broadcasted_iota(jnp.int32, (tokens, HD), 0) == lax.broadcasted_iota(
+        jnp.int32, (tokens, HD), 1
+    )
+    asked = ask_ref[pl.ds(tokens, CODES), pl.ds(0, HD)].astype(jnp.float32)[0:1]
+    doc = jnp.sum(jnp.where(square, asked, 0.0), axis=1, keepdims=True)
     row_doc = jnp.concatenate([jnp.broadcast_to(doc, (tokens, HD))] * GROUPS, axis=0)
     scale = to_log2 * HD ** (-0.5)
 
     def body(b, carry):
         rows = pl.ds(pl.multiple_of(b * block, block), block)
         wide = pl.ds(pl.multiple_of(b * GROUPS * HD, GROUPS * HD), GROUPS * HD)
-        q = queries_ref[:, wide]
+        q = ask_ref[pl.ds(0, tokens), wide]
         q = jnp.concatenate([q[:, g * HD : (g + 1) * HD] for g in range(GROUPS)], axis=0)
         tiles = []
         for ref, h in halves:
@@ -138,7 +163,7 @@
         ]
         late = contract_last(q, new_keys)
         seen = row_fresh == row_doc
-        if own:
+        if first and mine:
             token = lax.broadcasted_iota(jnp.int32, (block, HD), 0) % tokens
             seen = seen & (lax.broadcasted_iota(jnp.int32, (block, HD), 1) <= token)
         tiles.append(jnp.where(seen, late * scale, masked_score))
@@ -146,7 +171,7 @@
         for t in tiles[1:]:
             top = jnp.maximum(top, t)
         top = jnp.max(top, axis=1, keepdims=True)
-        if own:
+        if first:
             top = jnp.broadcast_to(top, (block, HD))
         else:
             before = state[1][rows, :]
@@ -161,46 +186,59 @@
         for n, (ref, h) in enumerate(halves):
             part = jnp.concatenate(weights[n * each : (n + 1) * each], axis=1)
             summed = summed + dot(part, ref[h, pl.ds(slots, slots), :])
-        if not own:
+        if not first:
             total = total + state[2][rows, :] * fade
             summed = summed + state[0][rows, :] * fade
         if last:
-            value = (summed / jnp.sum(total, axis=1, keepdims=True)).astype(jnp.bfloat16)
-            value = jnp.concatenate(
-                [value[g * tokens : (g + 1) * tokens] for g in range(GROUPS)], axis=1
-            )
-            for copy in range(outs[0].shape[0]):
-                outs[0][copy, :, wide] = value
+            total = jnp.sum(total, axis=1, keepdims=True)
+            outs[0][rows, :] = (summed / total).astype(jnp.bfloat16)
+            level = top + jnp.log(total) * to_log2
+            for i in range(block // HD):
+                flat = level[i * HD : (i + 1) * HD].T
+                outs[1][pl.ds(b * (block // HD) + i, 1), :] = flat[0:1]
         else:
             outs[0][rows, :] = summed
             outs[1][rows, :] = top
             outs[2][rows, :] = total
         return carry
 
+    if last:
+        outs[1][...] = jnp.zeros(outs[1].shape, jnp.float32)
     lax.fori_loop(0, width // (GROUPS * HD), body, 0)
-
-
-def attend(queries, doc, payloads, state, last=0):
-    tokens, width = queries.shape
+    if last:
+        level = outs[1][...]
+        high = level.astype(jnp.bfloat16).astype(jnp.float32)
+        middle = (level - high).astype(jnp.bfloat16).astype(jnp.float32)
+        low = level - high - middle
+        terms = jnp.concatenate([high, middle, low, low], axis=0).astype(jnp.bfloat16)
+        outs[0][pl.ds(width // (GROUPS * HD) * block, terms.shape[0]), :] = terms
+
+
+def attend(ask, payloads, state, mine, last=False):
+    width = ask.shape[1]
+    tokens = ask.shape[0] - CODES
     rows = tokens * width // HD
-    own = state is None
+    first = state is None
     many = len(payloads)
 
     def kernel(*refs):
-        attend_kernel(own, last, many, *refs)
-
+        attend_kernel(first, mine, last, many, *refs)
+
+    scratch = []
     if last:
-        out_shape = [jax.ShapeDtypeStruct((last, tokens, width), jnp.bfloat16)]
+        out_shape = [jax.ShapeDtypeStruct((rows + 4 * 8, HD), jnp.bfloat16)]
+        scratch = [pltpu.VMEM((8, HD), jnp.float32)]
     else:
         out_shape = [jax.ShapeDtypeStruct((rows, HD), jnp.float32)] * 3
-    args = (queries, doc, *payloads, *(() if own else state))
+    args = (ask, *payloads, *(() if first else state))
     keys = sum(p.shape[0] * p.shape[1] for p in payloads) // 2
     return pl.pallas_call(
         kernel,
         out_shape=out_shape,
         in_specs=[VMEM] * len(args),
         out_specs=[VMEM] * len(out_shape),
-        name="attend_last" if last else ("attend_own" if own else "attend_step"),
+        scratch_shapes=scratch,
+        name="attend_last" if last else ("attend_first" if first else "attend_step"),
         cost_estimate=pl.CostEstimate(
             flops=16 * rows * keys * HD,
             bytes_accessed=keys * HD * 4 + 6 * rows * HD * 4,
@@ -208,6 +246,38 @@
         ),
         compiler_params=pltpu.CompilerParams(vmem_limit_bytes=12 * 1024 * 1024),
     )(*args)
+
+
+def merge_kernel(summed_ref, top_ref, total_ref, other_ref, out_ref):
+    copies, tokens, _ = out_ref.shape
+    rows = summed_ref.shape[0]
+    terms = other_ref[pl.ds(rows, 4 * 8), :].astype(jnp.float32)
+    level = terms[0:8] + terms[8:16] + terms[16:24]
+    for i in range(rows // HD):
+        at = pl.ds(i * HD, HD)
+        other = jnp.broadcast_to(level[i : i + 1], (HD, HD)).T
+        top = jnp.maximum(top_ref[at, :], other)
+        mine = jnp.exp2(top_ref[at, :] - top)
+        theirs = jnp.exp2(other - top)
+        total = jnp.sum(total_ref[at, :], axis=1, keepdims=True) * mine + theirs
+        summed = summed_ref[at, :] * mine + other_ref[at, :].astype(jnp.float32) * theirs
+        value = (summed / total).astype(jnp.bfloat16)
+        for g in range(HD // tokens):
+            head = i * (HD // tokens) + g
+            for copy in range(copies):
+                out_ref[copy, :, pl.ds(head * HD, HD)] = value[g * tokens : (g + 1) * tokens]
+
+
+def merge(state, other, copies, tokens):
+    rows = state[0].shape[0]
+    return pl.pallas_call(
+        merge_kernel,
+        out_shape=jax.ShapeDtypeStruct((copies, tokens, rows // tokens * HD), jnp.bfloat16),
+        in_specs=[VMEM] * 4,
+        out_specs=VMEM,
+        name="merge",
+        compiler_params=pltpu.CompilerParams(vmem_limit_bytes=8 * 1024 * 1024),
+    )(*state, other)
 
 
 def project_kernel(a_ref, own_ref, other_ref, out_ref):
@@ -284,14 +354,21 @@
     fresh = queries.shape[1]
     width = queries.shape[2]
 
-    own = pack(
-        keep_lengths, cache_keys[0], cache_values[0], new_keys[0], new_values[0], cache_doc, new_doc
-    )
-    up = [(i, (i + 1) % ring) for i in range(ring)]
-    down = [(i, (i - 1) % ring) for i in range(ring)]
-
-    hops = ring // 2
-    state = None
+    own, ask = pack(
+        keep_lengths,
+        queries[0],
+        cache_keys[0],
+        cache_values[0],
+        new_keys[0],
+        new_values[0],
+        cache_doc,
+        new_doc,
+    )
+    up = [(i, (i + 2) % ring) for i in range(ring)]
+    down = [(i, (i - 2) % ring) for i in range(ring)]
+    pair = [(i, i + 1 - 2 * (i % 2)) for i in range(ring)]
+    hops = ring // 4
+    state = other = None
     below = above = own
     for s in range(hops + 1):
         chunks = [below, above] if s else [own]
@@ -301,9 +378,14 @@
             below = lax.ppermute(below, "seq", up)
             above = lax.ppermute(above, "seq", down)
             if s == 0:
+                asked = lax.ppermute(ask, "seq", pair)
                 other_weight = lax.ppermute(out_weight, "core", [(0, 1), (1, 0)])
-            state = attend(queries[0], new_doc, chunks, state)
-    (attended,) = attend(queries[0], new_doc, chunks, state, last=packs)
+            state = attend(ask, chunks, state, True)
+            other = attend(asked, chunks, other, False)
+    (other,) = attend(asked, chunks, other, False, last=True)
+    other = lax.ppermute(other, "seq", pair)
+    state = attend(ask, chunks, state, True)
+    attended = merge(state, other, packs, fresh)
 
     each = fresh // cores
     tiles = lax.all_to_all(

time: 146 us -> 138 us (0.945)
  starting transfers between devices: 65.5 us -> 55.9 us
  waiting for transfers between devices: 16.7 us -> 21.5 us
  local copies, waits for them, and re-layouts: 6.89 us -> 2.64 us
  Pallas kernels: 17 us -> 21 us
  blocking collectives: 38.1 us -> 35.1 us
    ppermute x8 -> x4, starting transfers between devices: 41.4 us -> 26.6 us  [local(): above = lax.ppermute(above, 'seq', down)]
    ppermute x0 -> x2, starting transfers between devices: none -> 12.9 us  [the longest x1 10.5 us: local(): other = lax.ppermute(other, 'seq', pair)]
    ppermute x0 -> x2, waiting for transfers between devices: none -> 10.4 us  [the longest x1 10.4 us: local(): asked = lax.ppermute(ask, 'seq', pair)]
    ppermute x8 -> x4, starting transfers between devices: 15.4 us -> 7.68 us  [local(): below = lax.ppermute(below, 'seq', up)]
    ppermute x8 -> x4, waiting for transfers between devices: 14.7 us -> 7.46 us  [local(): above = lax.ppermute(above, 'seq', down)]
    unnamed x18 -> x8, local copies, waits for them, and re-layouts: 6.13 us -> 1.88 us
    all_to_all x1, blocking collectives: 20.7 us -> 17.7 us  [local(): lax.all_to_all(attended.reshape(packs * cores, each, width), ('dp', 'core...]
    ppermute x8 -> x4, waiting for transfers between devices: 1.99 us -> 3.71 us  [local(): below = lax.ppermute(below, 'seq', up)]
  transfers between devices with their start and end apart: 17 -> 11, of which waited for: 6 -> 3; matrix products, arithmetic and copies ran while one was open for 0% -> 0% of each run, Pallas kernels for 10% -> 12%
where the time goes in v3:
time: 138 us; the launch traced here: 137 us
  starting transfers between devices  55.9 us (41%)
  blocking collectives  35.1 us (25%)
  waiting for transfers between devices  21.5 us (16%)
  Pallas kernels  21 us (15%)
  local copies, waits for them, and re-layouts  2.64 us (2%)
    ppermute x4, starting transfers between devices, local(): above = lax.ppermute(above, 'seq', down)  26.6 us
    all_to_all x1, blocking collectives, local(): lax.all_to_all(attended.reshape(packs * cores, each, width), ('dp', 'core...  17.7 us
    all_to_all x1, blocking collectives, local(): lax.all_to_all(pieces.reshape(packs * mesh_x * cores, each, cols), ('dp',...  17.3 us
    pallas_call x10, Pallas kernels, attend(): pl.pallas_call(kernel, out_shape=out_shape, in_specs=[VMEM] * len(args),...  14.5 us
    ppermute x1, starting transfers between devices, local(): other = lax.ppermute(other, 'seq', pair)  10.5 us
    ppermute x1, waiting for transfers between devices, local(): asked = lax.ppermute(ask, 'seq', pair)  10.4 us
    ppermute x1, starting transfers between devices, local(): other_weight = lax.ppermute(out_weight, 'core', [(0, 1), (1, 0)])  8.74 us
    ppermute x4, starting transfers between devices, local(): below = lax.ppermute(below, 'seq', up)  7.68 us
  transfers between devices with their start and end apart: 11, of which 3 were waited for; matrix products, arithmetic and copies ran while one was open for 0% of the time, Pallas kernels for 12%

profile of v3, /device:TPU:1, one launch (start us, length us, event | category | flops | bytes accessed | tf_op | source)
XLA Modules:
  0.0 137.0 jit_solution(7571522496778820676)
XLA Ops:
  0.0 8.7 %collective-permute-start.10 = (bf16[1024,2048]{1,0:T(8,128)(2,1)}, bf16[1024,2048]{1,0:T(8,128)(2,1)}, u32[]{:S(2)}, u32[]{:S(2)}) collective-permute-start(bf16[1024,2048]{1,0:T(8,128)(2,1)} %own_ref.1), channel_id=1, source_target_pairs={{0,1},{1,0},{2,3},{3,2},{4,5},{5,4},{6,7},{7,6},{8,9},{9,8},{10,11... | collective-permute-start | bytes 12582920 | tf_op jit(solution)/shard_map/ppermute | solution.py:382
  9.4 2.0 %pack.1 = (bf16[2,592,128]{2,1,0:T(8,128)(2,1)}, bf16[80,1024]{1,0:T(8,128)(2,1)}) custom-call(s32[1,1]{1,0:T(1,128)S(6)} %copy.10.keep_ref, bf16[64,1024]{1,0:T(8,128)(2,1)} %bitcast.13, bf16[512,128]{1,0:T(8,128)(2,1)} %bitcast.14, bf16[512,128]{1,0:T(8,128)(2,1)} %bitcast.15, bf16[64,128]{1,0:T(8,128)(2,1)} %bitcast.16, bf16[64,128]{1,0:T(8,128)(2,1)} %bitcast.17, ...), custom_call_target="tpu_custom_call" | custom-call | tf_op jit(solution)/shard_map/pack/pallas_call | solution.py:93
  11.4 6.2 %collective-permute-start.4 = (bf16[2,592,128]{2,1,0:T(8,128)(2,1)}, bf16[2,592,128]{2,1,0:T(8,128)(2,1)S(1)}, u32[]{:S(2)}, u32[]{:S(2)}) collective-permute-start(bf16[2,592,128]{2,1,0:T(8,128)(2,1)} %get-tuple-element.35.refs_1_), channel_id=1, source_target_pairs={{0,112},{8,120},{16,0},{24,8},{32,16},{40,24},{48,32},{56,40},{64,... | collective-permute-start | bytes 909320 | tf_op jit(solution)/shard_map/ppermute | solution.py:379
  17.6 1.9 %collective-permute-start = (bf16[2,592,128]{2,1,0:T(8,128)(2,1)}, bf16[2,592,128]{2,1,0:T(8,128)(2,1)S(1)}, u32[]{:S(2)}, u32[]{:S(2)}) collective-permute-start(bf16[2,592,128]{2,1,0:T(8,128)(2,1)} %get-tuple-element.35.refs_1_), channel_id=1, source_target_pairs={{0,16},{8,24},{16,32},{24,40},{32,48},{40,56},{48,64},{56,72},{64,... | collective-permute-start | bytes 909320 | tf_op jit(solution)/shard_map/ppermute | solution.py:378
  19.5 7.4 %collective-permute-done.4.refs_2_ = bf16[2,592,128]{2,1,0:T(8,128)(2,1)S(1)} collective-permute-done((bf16[2,592,128]{2,1,0:T(8,128)(2,1)}, bf16[2,592,128]{2,1,0:T(8,128)(2,1)S(1)}, u32[]{:S(2)}, u32[]{:S(2)}) %collective-permute-start.4) | collective-permute-done | bytes 303136 | tf_op jit(solution)/shard_map/ppermute | solution.py:379
  27.0 10.1 %collective-permute-start.5 = (bf16[2,592,128]{2,1,0:T(8,128)(2,1)S(1)}, bf16[2,592,128]{2,1,0:T(8,128)(2,1)S(1)}, u32[]{:S(2)}, u32[]{:S(2)}) collective-permute-start(bf16[2,592,128]{2,1,0:T(8,128)(2,1)S(1)} %collective-permute-done.4.refs_2_), channel_id=1, source_target_pairs={{0,112},{8,120},{16,0},{24,8},{32,16},{40,24},{48,32},{56,40},{64,... | collective-permute-start | bytes 909320 | tf_op jit(solution)/shard_map/ppermute | solution.py:379
  37.1 1.9 %collective-permute-start.1 = (bf16[2,592,128]{2,1,0:T(8,128)(2,1)S(1)}, bf16[2,592,128]{2,1,0:T(8,128)(2,1)S(1)}, u32[]{:S(2)}, u32[]{:S(2)}) collective-permute-start(bf16[2,592,128]{2,1,0:T(8,128)(2,1)S(1)} %collective-permute-done.refs_1_), channel_id=1, source_target_pairs={{0,16},{8,24},{16,32},{24,40},{32,48},{40,56},{48,64},{56,72},{64,... | collective-permute-start | bytes 909320 | tf_op jit(solution)/shard_map/ppermute | solution.py:378
  39.0 2.4 %collective-permute-start.8 = (bf16[80,1024]{1,0:T(8,128)(2,1)}, bf16[80,1024]{1,0:T(8,128)(2,1)S(1)}, u32[]{:S(2)}, u32[]{:S(2)}) collective-permute-start(bf16[80,1024]{1,0:T(8,128)(2,1)} %get-tuple-element.34.refs_0_), channel_id=1, source_target_pairs={{0,8},{8,0},{16,24},{24,16},{32,40},{40,32},{48,56},{56,48},{64,72... | collective-permute-start | bytes 491528 | tf_op jit(solution)/shard_map/ppermute | solution.py:381
  44.5 10.4 %collective-permute-done.8.refs_0_ = bf16[80,1024]{1,0:T(8,128)(2,1)S(1)} collective-permute-done((bf16[80,1024]{1,0:T(8,128)(2,1)}, bf16[80,1024]{1,0:T(8,128)(2,1)S(1)}, u32[]{:S(2)}, u32[]{:S(2)}) %collective-permute-start.8) | collective-permute-done | bytes 163872 | tf_op jit(solution)/shard_map/ppermute | solution.py:381
  56.2 4.8 %collective-permute-start.6 = (bf16[2,592,128]{2,1,0:T(8,128)(2,1)S(1)}, bf16[2,592,128]{2,1,0:T(8,128)(2,1)S(1)}, u32[]{:S(2)}, u32[]{:S(2)}) collective-permute-start(bf16[2,592,128]{2,1,0:T(8,128)(2,1)S(1)} %collective-permute-done.5.refs_2_), channel_id=1, source_target_pairs={{0,112},{8,120},{16,0},{24,8},{32,16},{40,24},{48,32},{56,40},{64,... | collective-permute-start | bytes 909320 | tf_op jit(solution)/shard_map/ppermute | solution.py:379
  61.0 1.9 %collective-permute-start.2 = (bf16[2,592,128]{2,1,0:T(8,128)(2,1)S(1)}, bf16[2,592,128]{2,1,0:T(8,128)(2,1)S(1)}, u32[]{:S(2)}, u32[]{:S(2)}) collective-permute-start(bf16[2,592,128]{2,1,0:T(8,128)(2,1)S(1)} %collective-permute-done.1.refs_1_), channel_id=1, source_target_pairs={{0,16},{8,24},{16,32},{24,40},{32,48},{40,56},{48,64},{56,72},{64,... | collective-permute-start | bytes 909320 | tf_op jit(solution)/shard_map/ppermute | solution.py:378
  62.9 1.6 %attend_step.11 = (f32[512,128]{1,0:T(8,128)S(1)}, f32[512,128]{1,0:T(8,128)S(1)}, f32[512,128]{1,0:T(8,128)S(1)}) custom-call(bf16[80,1024]{1,0:T(8,128)(2,1)S(1)} %collective-permute-done.8.refs_0_, bf16[2,592,128]{2,1,0:T(8,128)(2,1)S(1)} %collective-permute-done.refs_1_, bf16[2,592,128]{2,1,0:T(8,128)(2,1)S(1)} %collective-permute-done.4.refs_2_, ...), custom_call_target="tpu_custom_call" | custom-call | flops 1241513984 | bytes 2179072 | tf_op jit(solution)/shard_map/attend_step/pallas_call | solution.py:235
  64.5 1.6 %attend_step.7 = (f32[512,128]{1,0:T(8,128)S(1)}, f32[512,128]{1,0:T(8,128)S(1)}, f32[512,128]{1,0:T(8,128)S(1)}) custom-call(bf16[80,1024]{1,0:T(8,128)(2,1)S(1)} %copy-done.3, bf16[2,592,128]{2,1,0:T(8,128)(2,1)S(1)} %collective-permute-done.refs_1_, bf16[2,592,128]{2,1,0:T(8,128)(2,1)S(1)} %collective-permute-done.4.refs_2_, ...), custom_call_target="tpu_custom_call" | custom-call | flops 1241513984 | bytes 2179072 | tf_op jit(solution)/shard_map/attend_step/pallas_call | solution.py:235
  66.1 1.6 %attend_step.12 = (f32[512,128]{1,0:T(8,128)S(1)}, f32[512,128]{1,0:T(8,128)S(1)}, f32[512,128]{1,0:T(8,128)S(1)}) custom-call(bf16[80,1024]{1,0:T(8,128)(2,1)S(1)} %collective-permute-done.8.refs_0_, bf16[2,592,128]{2,1,0:T(8,128)(2,1)S(1)} %collective-permute-done.1.refs_1_, bf16[2,592,128]{2,1,0:T(8,128)(2,1)S(1)} %collective-permute-done.5.refs_2_, ...), custom_call_target="tpu_custom_call" | custom-call | flops 1241513984 | bytes 2179072 | tf_op jit(solution)/shard_map/attend_step/pallas_call | solution.py:235
  67.7 5.5 %collective-permute-start.7 = (bf16[1,592,128]{2,1,0:T(8,128)(2,1)S(1)}, bf16[1,592,128]{2,1,0:T(8,128)(2,1)S(1)}, u32[]{:S(2)}, u32[]{:S(2)}) collective-permute-start(bf16[1,592,128]{2,1,0:T(8,128)(2,1)S(1)} %slice.9), channel_id=1, source_target_pairs={{0,112},{8,120},{16,0},{24,8},{32,16},{40,24},{48,32},{56,40},{64,... | collective-permute-start | bytes 454664 | tf_op jit(solution)/shard_map/ppermute | solution.py:379
  73.2 1.9 %collective-permute-start.3 = (bf16[1,592,128]{2,1,0:T(8,128)(2,1)S(1)}, bf16[1,592,128]{2,1,0:T(8,128)(2,1)S(1)}, u32[]{:S(2)}, u32[]{:S(2)}) collective-permute-start(bf16[1,592,128]{2,1,0:T(8,128)(2,1)S(1)} %slice.8), channel_id=1, source_target_pairs={{0,16},{8,24},{16,32},{24,40},{32,48},{40,56},{48,64},{56,72},{64,... | collective-permute-start | bytes 454664 | tf_op jit(solution)/shard_map/ppermute | solution.py:378
  75.2 1.6 %attend_step.8 = (f32[512,128]{1,0:T(8,128)S(1)}, f32[512,128]{1,0:T(8,128)S(1)}, f32[512,128]{1,0:T(8,128)S(1)}) custom-call(bf16[80,1024]{1,0:T(8,128)(2,1)S(1)} %copy-done.3, bf16[2,592,128]{2,1,0:T(8,128)(2,1)S(1)} %collective-permute-done.1.refs_1_, bf16[2,592,128]{2,1,0:T(8,128)(2,1)S(1)} %collective-permute-done.5.refs_2_, ...), custom_call_target="tpu_custom_call" | custom-call | flops 1241513984 | bytes 2179072 | tf_op jit(solution)/shard_map/attend_step/pallas_call | solution.py:235
  76.7 1.6 %attend_step.13 = (f32[512,128]{1,0:T(8,128)S(1)}, f32[512,128]{1,0:T(8,128)S(1)}, f32[512,128]{1,0:T(8,128)S(1)}) custom-call(bf16[80,1024]{1,0:T(8,128)(2,1)S(1)} %collective-permute-done.8.refs_0_, bf16[2,592,128]{2,1,0:T(8,128)(2,1)S(1)} %collective-permute-done.2.refs_1_, bf16[2,592,128]{2,1,0:T(8,128)(2,1)S(1)} %collective-permute-done.6.refs_2_, ...), custom_call_target="tpu_custom_call" | custom-call | flops 1241513984 | bytes 2179072 | tf_op jit(solution)/shard_map/attend_step/pallas_call | solution.py:235
  78.3 3.7 %collective-permute-done.3.refs_1_ = bf16[1,592,128]{2,1,0:T(8,128)(2,1)S(1)} collective-permute-done((bf16[1,592,128]{2,1,0:T(8,128)(2,1)S(1)}, bf16[1,592,128]{2,1,0:T(8,128)(2,1)S(1)}, u32[]{:S(2)}, u32[]{:S(2)}) %collective-permute-start.3) | collective-permute-done | bytes 151584 | tf_op jit(solution)/shard_map/ppermute | solution.py:378
  83.3 10.5 %collective-permute-start.9 = (bf16[544,128]{1,0:T(8,128)(2,1)S(1)}, bf16[544,128]{1,0:T(8,128)(2,1)S(1)}, u32[]{:S(2)}, u32[]{:S(2)}) collective-permute-start(bf16[544,128]{1,0:T(8,128)(2,1)S(1)} %attend_last.1), channel_id=1, source_target_pairs={{0,8},{8,0},{16,24},{24,16},{32,40},{40,32},{48,56},{56,48},{64,72... | collective-permute-start | bytes 417800 | tf_op jit(solution)/shard_map/ppermute | solution.py:386
  93.8 1.6 %attend_step.9 = (f32[512,128]{1,0:T(8,128)S(1)}, f32[512,128]{1,0:T(8,128)S(1)}, f32[512,128]{1,0:T(8,128)S(1)}) custom-call(bf16[80,1024]{1,0:T(8,128)(2,1)S(1)} %copy-done.3, bf16[2,592,128]{2,1,0:T(8,128)(2,1)S(1)} %collective-permute-done.2.refs_1_, bf16[2,592,128]{2,1,0:T(8,128)(2,1)S(1)} %collective-permute-done.6.refs_2_, ...), custom_call_target="tpu_custom_call" | custom-call | flops 1241513984 | bytes 2179072 | tf_op jit(solution)/shard_map/attend_step/pallas_call | solution.py:235
  96.9 17.7 %all_to_all.10 = bf16[8,32,1024]{2,1,0:T(8,128)(2,1)S(1)} all-to-all(bf16[8,32,1024]{2,1,0:T(8,128)(2,1)S(1)} %bitcast.12), channel_id=1, replica_groups=mesh['dp'=4,'seq'=16,'x'=4,'core'=2] {'dp','core'}, dimensions={0} | all-to-all | bytes 1048576 | tf_op jit(solution)/shard_map/all_to_all | solution.py:391
  114.6 4.2 %project.1 = bf16[4,8,32,256]{3,2,1,0:T(8,128)(2,1)S(1)} custom-call(bf16[4,2,32,1024]{3,2,1,0:T(8,128)(2,1)S(1)} %bitcast.9, bf16[1024,2048]{1,0:T(8,128)(2,1)S(1)} %copy-done, bf16[1024,2048]{1,0:T(8,128)(2,1)} %collective-permute-done.10.other_ref), custom_call_target="tpu_custom_call" | custom-call | flops 1073741824 | bytes 8388608 | tf_op jit(solution)/shard_map/project/pallas_call | solution.py:299
  118.8 17.3 %all_to_all.11 = bf16[32,32,256]{2,1,0:T(8,128)(2,1)S(1)} all-to-all(bf16[32,32,256]{2,1,0:T(8,128)(2,1)S(1)} %bitcast.10), channel_id=1, replica_groups=mesh['dp'=4,'seq'=16,'x'=4,'core'=2] {'dp','x','core'}, dimensions={0} | all-to-all | bytes 1048576 | tf_op jit(solution)/shard_map/all_to_all | solution.py:396
  (25 shorter events, 7.9 us)
Async XLA Ops:
  0.0 114.6 %collective-permute-start.10 = (bf16[1024,2048]{1,0:T(8,128)(2,1)}, bf16[1024,2048]{1,0:T(8,128)(2,1)}, u32[]{:S(2)}, u32[]{:S(2)}) collective-permute-start(bf16[1024,2048]{1,0:T(8,128)(2,1)} %own_ref.1), channel_id=1, source_target_pairs={{0,1},{1,0},{2,3},{3,2},{4,5},{5,4},{6,7},{7,6},{8,9},{9,8},{10,11... | collective-permute-start | bytes 12582920 | tf_op jit(solution)/shard_map/ppermute | solution.py:382
  11.4 15.6 %collective-permute-start.4 = (bf16[2,592,128]{2,1,0:T(8,128)(2,1)}, bf16[2,592,128]{2,1,0:T(8,128)(2,1)S(1)}, u32[]{:S(2)}, u32[]{:S(2)}) collective-permute-start(bf16[2,592,128]{2,1,0:T(8,128)(2,1)} %get-tuple-element.35.refs_1_), channel_id=1, source_target_pairs={{0,112},{8,120},{16,0},{24,8},{32,16},{40,24},{48,32},{56,40},{64,... | collective-permute-start | bytes 909320 | tf_op jit(solution)/shard_map/ppermute | solution.py:379
  17.6 19.5 %collective-permute-start = (bf16[2,592,128]{2,1,0:T(8,128)(2,1)}, bf16[2,592,128]{2,1,0:T(8,128)(2,1)S(1)}, u32[]{:S(2)}, u32[]{:S(2)}) collective-permute-start(bf16[2,592,128]{2,1,0:T(8,128)(2,1)} %get-tuple-element.35.refs_1_), channel_id=1, source_target_pairs={{0,16},{8,24},{16,32},{24,40},{32,48},{40,56},{48,64},{56,72},{64,... | collective-permute-start | bytes 909320 | tf_op jit(solution)/shard_map/ppermute | solution.py:378
  27.0 29.2 %collective-permute-start.5 = (bf16[2,592,128]{2,1,0:T(8,128)(2,1)S(1)}, bf16[2,592,128]{2,1,0:T(8,128)(2,1)S(1)}, u32[]{:S(2)}, u32[]{:S(2)}) collective-permute-start(bf16[2,592,128]{2,1,0:T(8,128)(2,1)S(1)} %collective-permute-done.4.refs_2_), channel_id=1, source_target_pairs={{0,112},{8,120},{16,0},{24,8},{32,16},{40,24},{48,32},{56,40},{64,... | collective-permute-start | bytes 909320 | tf_op jit(solution)/shard_map/ppermute | solution.py:379
  37.1 23.9 %collective-permute-start.1 = (bf16[2,592,128]{2,1,0:T(8,128)(2,1)S(1)}, bf16[2,592,128]{2,1,0:T(8,128)(2,1)S(1)}, u32[]{:S(2)}, u32[]{:S(2)}) collective-permute-start(bf16[2,592,128]{2,1,0:T(8,128)(2,1)S(1)} %collective-permute-done.refs_1_), channel_id=1, source_target_pairs={{0,16},{8,24},{16,32},{24,40},{32,48},{40,56},{48,64},{56,72},{64,... | collective-permute-start | bytes 909320 | tf_op jit(solution)/shard_map/ppermute | solution.py:378
  39.0 15.9 %collective-permute-start.8 = (bf16[80,1024]{1,0:T(8,128)(2,1)}, bf16[80,1024]{1,0:T(8,128)(2,1)S(1)}, u32[]{:S(2)}, u32[]{:S(2)}) collective-permute-start(bf16[80,1024]{1,0:T(8,128)(2,1)} %get-tuple-element.34.refs_0_), channel_id=1, source_target_pairs={{0,8},{8,0},{16,24},{24,16},{32,40},{40,32},{48,56},{56,48},{64,72... | collective-permute-start | bytes 491528 | tf_op jit(solution)/shard_map/ppermute | solution.py:381
  41.4 1.0 copy-start.1
  42.4 0.9 copy-start.2
  43.3 21.2 %copy-start.3 = (bf16[80,1024]{1,0:T(8,128)(2,1)S(1)}, bf16[80,1024]{1,0:T(8,128)(2,1)}, u32[]{:S(2)}) copy-start(bf16[80,1024]{1,0:T(8,128)(2,1)} %get-tuple-element.34.refs_0_) | copy-start | bytes 491524
  56.2 11.5 %collective-permute-start.6 = (bf16[2,592,128]{2,1,0:T(8,128)(2,1)S(1)}, bf16[2,592,128]{2,1,0:T(8,128)(2,1)S(1)}, u32[]{:S(2)}, u32[]{:S(2)}) collective-permute-start(bf16[2,592,128]{2,1,0:T(8,128)(2,1)S(1)} %collective-permute-done.5.refs_2_), channel_id=1, source_target_pairs={{0,112},{8,120},{16,0},{24,8},{32,16},{40,24},{48,32},{56,40},{64,... | collective-permute-start | bytes 909320 | tf_op jit(solution)/shard_map/ppermute | solution.py:379
  61.0 12.2 %collective-permute-start.2 = (bf16[2,592,128]{2,1,0:T(8,128)(2,1)S(1)}, bf16[2,592,128]{2,1,0:T(8,128)(2,1)S(1)}, u32[]{:S(2)}, u32[]{:S(2)}) collective-permute-start(bf16[2,592,128]{2,1,0:T(8,128)(2,1)S(1)} %collective-permute-done.1.refs_1_), channel_id=1, source_target_pairs={{0,16},{8,24},{16,32},{24,40},{32,48},{40,56},{48,64},{56,72},{64,... | collective-permute-start | bytes 909320 | tf_op jit(solution)/shard_map/ppermute | solution.py:378
  67.7 10.6 %collective-permute-start.7 = (bf16[1,592,128]{2,1,0:T(8,128)(2,1)S(1)}, bf16[1,592,128]{2,1,0:T(8,128)(2,1)S(1)}, u32[]{:S(2)}, u32[]{:S(2)}) collective-permute-start(bf16[1,592,128]{2,1,0:T(8,128)(2,1)S(1)} %slice.9), channel_id=1, source_target_pairs={{0,112},{8,120},{16,0},{24,8},{32,16},{40,24},{48,32},{56,40},{64,... | collective-permute-start | bytes 454664 | tf_op jit(solution)/shard_map/ppermute | solution.py:379
  73.2 8.8 %collective-permute-start.3 = (bf16[1,592,128]{2,1,0:T(8,128)(2,1)S(1)}, bf16[1,592,128]{2,1,0:T(8,128)(2,1)S(1)}, u32[]{:S(2)}, u32[]{:S(2)}) collective-permute-start(bf16[1,592,128]{2,1,0:T(8,128)(2,1)S(1)} %slice.8), channel_id=1, source_target_pairs={{0,16},{8,24},{16,32},{24,40},{32,48},{40,56},{48,64},{56,72},{64,... | collective-permute-start | bytes 454664 | tf_op jit(solution)/shard_map/ppermute | solution.py:378
  83.3 13.4 %collective-permute-start.9 = (bf16[544,128]{1,0:T(8,128)(2,1)S(1)}, bf16[544,128]{1,0:T(8,128)(2,1)S(1)}, u32[]{:S(2)}, u32[]{:S(2)}) collective-permute-start(bf16[544,128]{1,0:T(8,128)(2,1)S(1)} %attend_last.1), channel_id=1, source_target_pairs={{0,8},{8,0},{16,24},{24,16},{32,40},{40,32},{48,56},{56,48},{64,72... | collective-permute-start | bytes 417800 | tf_op jit(solution)/shard_map/ppermute | solution.py:386
  93.8 20.8 %copy-start = (bf16[1024,2048]{1,0:T(8,128)(2,1)S(1)}, bf16[1024,2048]{1,0:T(8,128)(2,1)}, u32[]{:S(2)}) copy-start(bf16[1024,2048]{1,0:T(8,128)(2,1)} %own_ref.1) | copy-start | bytes 12582916

commit v4 on v3

--- a/solution.py
+++ b/solution.py
@@ -317,20 +317,22 @@
 
 
 def gather_sum_kernel(parts_ref, out_ref):
-    packs, terms, cores, each, cols = parts_ref.shape
-    for d in range(packs):
-        for c in range(cores):
+    packs, terms, cores, each, _ = parts_ref.shape
+    for c in range(cores):
+        blocks = []
+        for d in range(packs):
             total = parts_ref[d, 0, c].astype(jnp.float32)
             for t in range(1, terms):
                 total = total + parts_ref[d, t, c].astype(jnp.float32)
-            out_ref[pl.ds(c * each, each), pl.ds(d * cols, cols)] = total.astype(jnp.bfloat16)
+            blocks.append(total)
+        out_ref[pl.ds(c * each, each)] = jnp.stack(blocks, axis=1).astype(jnp.bfloat16)
 
 
 def gather_sum(parts):
     packs, _, cores, each, cols = parts.shape
     return pl.pallas_call(
         gather_sum_kernel,
-        out_shape=jax.ShapeDtypeStruct((cores * each, packs * cols), jnp.bfloat16),
+        out_shape=jax.ShapeDtypeStruct((cores * each, packs, cols), jnp.bfloat16),
         in_specs=[VMEM],
         out_specs=VMEM,
         name="gather_sum",
@@ -397,7 +399,7 @@
         pieces.reshape(packs * mesh_x * cores, each, cols), ("dp", "x", "core"), 0, 0, tiled=True
     )
     result = gather_sum(arrived.reshape(packs, mesh_x, cores, each, cols))
-    return result.reshape(1, fresh, packs, cols)
+    return result[None]
 
 
 def solution(mesh):

time: 138 us -> 138 us (level)
  no operation moved by 1% of the time
where the time goes in v4:
time: 138 us; the launch traced here: 137 us
  starting transfers between devices  55.9 us (41%)
  blocking collectives  35.1 us (25%)
  Pallas kernels  21.8 us (16%)
  waiting for transfers between devices  21.5 us (16%)
  local copies, waits for them, and re-layouts  1.91 us (1%)
    ppermute x4, starting transfers between devices, local(): above = lax.ppermute(above, 'seq', down)  26.6 us
    all_to_all x1, blocking collectives, local(): lax.all_to_all(attended.reshape(packs * cores, each, width), ('dp', 'core...  17.7 us
    all_to_all x1, blocking collectives, local(): lax.all_to_all(pieces.reshape(packs * mesh_x * cores, each, cols), ('dp',...  17.3 us
    pallas_call x10, Pallas kernels, attend(): pl.pallas_call(kernel, out_shape=out_shape, in_specs=[VMEM] * len(args),...  14.5 us
    ppermute x1, starting transfers between devices, local(): other = lax.ppermute(other, 'seq', pair)  10.5 us
    ppermute x1, waiting for transfers between devices, local(): asked = lax.ppermute(ask, 'seq', pair)  10.4 us
    ppermute x1, starting transfers between devices, local(): other_weight = lax.ppermute(out_weight, 'core', [(0, 1), (1, 0)])  8.74 us
    ppermute x4, starting transfers between devices, local(): below = lax.ppermute(below, 'seq', up)  7.68 us
  transfers between devices with their start and end apart: 11, of which 3 were waited for; matrix products, arithmetic and copies ran while one was open for 0% of the time, Pallas kernels for 12%

profile of v4, /device:TPU:1, one launch (start us, length us, event | category | flops | bytes accessed | tf_op | source)
XLA Modules:
  0.0 137.1 jit_solution(16735179308784314118)
XLA Ops:
  0.0 8.7 %collective-permute-start.10 = (bf16[1024,2048]{1,0:T(8,128)(2,1)}, bf16[1024,2048]{1,0:T(8,128)(2,1)}, u32[]{:S(2)}, u32[]{:S(2)}) collective-permute-start(bf16[1024,2048]{1,0:T(8,128)(2,1)} %own_ref.1), channel_id=1, source_target_pairs={{0,1},{1,0},{2,3},{3,2},{4,5},{5,4},{6,7},{7,6},{8,9},{9,8},{10,11... | collective-permute-start | bytes 12582920 | tf_op jit(solution)/shard_map/ppermute | solution.py:384
  9.4 2.0 %pack.1 = (bf16[2,592,128]{2,1,0:T(8,128)(2,1)}, bf16[80,1024]{1,0:T(8,128)(2,1)}) custom-call(s32[1,1]{1,0:T(1,128)S(6)} %copy.10.keep_ref, bf16[64,1024]{1,0:T(8,128)(2,1)} %bitcast.14, bf16[512,128]{1,0:T(8,128)(2,1)} %bitcast.15, bf16[512,128]{1,0:T(8,128)(2,1)} %bitcast.16, bf16[64,128]{1,0:T(8,128)(2,1)} %bitcast.17, bf16[64,128]{1,0:T(8,128)(2,1)} %bitcast.18, ...), custom_call_target="tpu_custom_call" | custom-call | tf_op jit(solution)/shard_map/pack/pallas_call | solution.py:93
  11.4 6.2 %collective-permute-start.4 = (bf16[2,592,128]{2,1,0:T(8,128)(2,1)}, bf16[2,592,128]{2,1,0:T(8,128)(2,1)S(1)}, u32[]{:S(2)}, u32[]{:S(2)}) collective-permute-start(bf16[2,592,128]{2,1,0:T(8,128)(2,1)} %get-tuple-element.35.refs_1_), channel_id=1, source_target_pairs={{0,112},{8,120},{16,0},{24,8},{32,16},{40,24},{48,32},{56,40},{64,... | collective-permute-start | bytes 909320 | tf_op jit(solution)/shard_map/ppermute | solution.py:381
  17.6 1.9 %collective-permute-start = (bf16[2,592,128]{2,1,0:T(8,128)(2,1)}, bf16[2,592,128]{2,1,0:T(8,128)(2,1)S(1)}, u32[]{:S(2)}, u32[]{:S(2)}) collective-permute-start(bf16[2,592,128]{2,1,0:T(8,128)(2,1)} %get-tuple-element.35.refs_1_), channel_id=1, source_target_pairs={{0,16},{8,24},{16,32},{24,40},{32,48},{40,56},{48,64},{56,72},{64,... | collective-permute-start | bytes 909320 | tf_op jit(solution)/shard_map/ppermute | solution.py:380
  19.5 7.4 %collective-permute-done.4.refs_2_ = bf16[2,592,128]{2,1,0:T(8,128)(2,1)S(1)} collective-permute-done((bf16[2,592,128]{2,1,0:T(8,128)(2,1)}, bf16[2,592,128]{2,1,0:T(8,128)(2,1)S(1)}, u32[]{:S(2)}, u32[]{:S(2)}) %collective-permute-start.4) | collective-permute-done | bytes 303136 | tf_op jit(solution)/shard_map/ppermute | solution.py:381
  27.0 10.1 %collective-permute-start.5 = (bf16[2,592,128]{2,1,0:T(8,128)(2,1)S(1)}, bf16[2,592,128]{2,1,0:T(8,128)(2,1)S(1)}, u32[]{:S(2)}, u32[]{:S(2)}) collective-permute-start(bf16[2,592,128]{2,1,0:T(8,128)(2,1)S(1)} %collective-permute-done.4.refs_2_), channel_id=1, source_target_pairs={{0,112},{8,120},{16,0},{24,8},{32,16},{40,24},{48,32},{56,40},{64,... | collective-permute-start | bytes 909320 | tf_op jit(solution)/shard_map/ppermute | solution.py:381
  37.1 1.9 %collective-permute-start.1 = (bf16[2,592,128]{2,1,0:T(8,128)(2,1)S(1)}, bf16[2,592,128]{2,1,0:T(8,128)(2,1)S(1)}, u32[]{:S(2)}, u32[]{:S(2)}) collective-permute-start(bf16[2,592,128]{2,1,0:T(8,128)(2,1)S(1)} %collective-permute-done.refs_1_), channel_id=1, source_target_pairs={{0,16},{8,24},{16,32},{24,40},{32,48},{40,56},{48,64},{56,72},{64,... | collective-permute-start | bytes 909320 | tf_op jit(solution)/shard_map/ppermute | solution.py:380
  39.0 2.4 %collective-permute-start.8 = (bf16[80,1024]{1,0:T(8,128)(2,1)}, bf16[80,1024]{1,0:T(8,128)(2,1)S(1)}, u32[]{:S(2)}, u32[]{:S(2)}) collective-permute-start(bf16[80,1024]{1,0:T(8,128)(2,1)} %get-tuple-element.34.refs_0_), channel_id=1, source_target_pairs={{0,8},{8,0},{16,24},{24,16},{32,40},{40,32},{48,56},{56,48},{64,72... | collective-permute-start | bytes 491528 | tf_op jit(solution)/shard_map/ppermute | solution.py:383
  44.5 10.4 %collective-permute-done.8.refs_0_ = bf16[80,1024]{1,0:T(8,128)(2,1)S(1)} collective-permute-done((bf16[80,1024]{1,0:T(8,128)(2,1)}, bf16[80,1024]{1,0:T(8,128)(2,1)S(1)}, u32[]{:S(2)}, u32[]{:S(2)}) %collective-permute-start.8) | collective-permute-done | bytes 163872 | tf_op jit(solution)/shard_map/ppermute | solution.py:383
  56.2 4.8 %collective-permute-start.6 = (bf16[2,592,128]{2,1,0:T(8,128)(2,1)S(1)}, bf16[2,592,128]{2,1,0:T(8,128)(2,1)S(1)}, u32[]{:S(2)}, u32[]{:S(2)}) collective-permute-start(bf16[2,592,128]{2,1,0:T(8,128)(2,1)S(1)} %collective-permute-done.5.refs_2_), channel_id=1, source_target_pairs={{0,112},{8,120},{16,0},{24,8},{32,16},{40,24},{48,32},{56,40},{64,... | collective-permute-start | bytes 909320 | tf_op jit(solution)/shard_map/ppermute | solution.py:381
  61.0 1.9 %collective-permute-start.2 = (bf16[2,592,128]{2,1,0:T(8,128)(2,1)S(1)}, bf16[2,592,128]{2,1,0:T(8,128)(2,1)S(1)}, u32[]{:S(2)}, u32[]{:S(2)}) collective-permute-start(bf16[2,592,128]{2,1,0:T(8,128)(2,1)S(1)} %collective-permute-done.1.refs_1_), channel_id=1, source_target_pairs={{0,16},{8,24},{16,32},{24,40},{32,48},{40,56},{48,64},{56,72},{64,... | collective-permute-start | bytes 909320 | tf_op jit(solution)/shard_map/ppermute | solution.py:380
  62.9 1.6 %attend_step.11 = (f32[512,128]{1,0:T(8,128)S(1)}, f32[512,128]{1,0:T(8,128)S(1)}, f32[512,128]{1,0:T(8,128)S(1)}) custom-call(bf16[80,1024]{1,0:T(8,128)(2,1)S(1)} %collective-permute-done.8.refs_0_, bf16[2,592,128]{2,1,0:T(8,128)(2,1)S(1)} %collective-permute-done.refs_1_, bf16[2,592,128]{2,1,0:T(8,128)(2,1)S(1)} %collective-permute-done.4.refs_2_, ...), custom_call_target="tpu_custom_call" | custom-call | flops 1241513984 | bytes 2179072 | tf_op jit(solution)/shard_map/attend_step/pallas_call | solution.py:235
  64.5 1.6 %attend_step.7 = (f32[512,128]{1,0:T(8,128)S(1)}, f32[512,128]{1,0:T(8,128)S(1)}, f32[512,128]{1,0:T(8,128)S(1)}) custom-call(bf16[80,1024]{1,0:T(8,128)(2,1)S(1)} %copy-done.3, bf16[2,592,128]{2,1,0:T(8,128)(2,1)S(1)} %collective-permute-done.refs_1_, bf16[2,592,128]{2,1,0:T(8,128)(2,1)S(1)} %collective-permute-done.4.refs_2_, ...), custom_call_target="tpu_custom_call" | custom-call | flops 1241513984 | bytes 2179072 | tf_op jit(solution)/shard_map/attend_step/pallas_call | solution.py:235
  66.1 1.6 %attend_step.12 = (f32[512,128]{1,0:T(8,128)S(1)}, f32[512,128]{1,0:T(8,128)S(1)}, f32[512,128]{1,0:T(8,128)S(1)}) custom-call(bf16[80,1024]{1,0:T(8,128)(2,1)S(1)} %collective-permute-done.8.refs_0_, bf16[2,592,128]{2,1,0:T(8,128)(2,1)S(1)} %collective-permute-done.1.refs_1_, bf16[2,592,128]{2,1,0:T(8,128)(2,1)S(1)} %collective-permute-done.5.refs_2_, ...), custom_call_target="tpu_custom_call" | custom-call | flops 1241513984 | bytes 2179072 | tf_op jit(solution)/shard_map/attend_step/pallas_call | solution.py:235
  67.7 5.5 %collective-permute-start.7 = (bf16[1,592,128]{2,1,0:T(8,128)(2,1)S(1)}, bf16[1,592,128]{2,1,0:T(8,128)(2,1)S(1)}, u32[]{:S(2)}, u32[]{:S(2)}) collective-permute-start(bf16[1,592,128]{2,1,0:T(8,128)(2,1)S(1)} %slice.9), channel_id=1, source_target_pairs={{0,112},{8,120},{16,0},{24,8},{32,16},{40,24},{48,32},{56,40},{64,... | collective-permute-start | bytes 454664 | tf_op jit(solution)/shard_map/ppermute | solution.py:381
  73.2 1.9 %collective-permute-start.3 = (bf16[1,592,128]{2,1,0:T(8,128)(2,1)S(1)}, bf16[1,592,128]{2,1,0:T(8,128)(2,1)S(1)}, u32[]{:S(2)}, u32[]{:S(2)}) collective-permute-start(bf16[1,592,128]{2,1,0:T(8,128)(2,1)S(1)} %slice.8), channel_id=1, source_target_pairs={{0,16},{8,24},{16,32},{24,40},{32,48},{40,56},{48,64},{56,72},{64,... | collective-permute-start | bytes 454664 | tf_op jit(solution)/shard_map/ppermute | solution.py:380
  75.2 1.6 %attend_step.8 = (f32[512,128]{1,0:T(8,128)S(1)}, f32[512,128]{1,0:T(8,128)S(1)}, f32[512,128]{1,0:T(8,128)S(1)}) custom-call(bf16[80,1024]{1,0:T(8,128)(2,1)S(1)} %copy-done.3, bf16[2,592,128]{2,1,0:T(8,128)(2,1)S(1)} %collective-permute-done.1.refs_1_, bf16[2,592,128]{2,1,0:T(8,128)(2,1)S(1)} %collective-permute-done.5.refs_2_, ...), custom_call_target="tpu_custom_call" | custom-call | flops 1241513984 | bytes 2179072 | tf_op jit(solution)/shard_map/attend_step/pallas_call | solution.py:235
  76.7 1.6 %attend_step.13 = (f32[512,128]{1,0:T(8,128)S(1)}, f32[512,128]{1,0:T(8,128)S(1)}, f32[512,128]{1,0:T(8,128)S(1)}) custom-call(bf16[80,1024]{1,0:T(8,128)(2,1)S(1)} %collective-permute-done.8.refs_0_, bf16[2,592,128]{2,1,0:T(8,128)(2,1)S(1)} %collective-permute-done.2.refs_1_, bf16[2,592,128]{2,1,0:T(8,128)(2,1)S(1)} %collective-permute-done.6.refs_2_, ...), custom_call_target="tpu_custom_call" | custom-call | flops 1241513984 | bytes 2179072 | tf_op jit(solution)/shard_map/attend_step/pallas_call | solution.py:235
  78.3 3.7 %collective-permute-done.3.refs_1_ = bf16[1,592,128]{2,1,0:T(8,128)(2,1)S(1)} collective-permute-done((bf16[1,592,128]{2,1,0:T(8,128)(2,1)S(1)}, bf16[1,592,128]{2,1,0:T(8,128)(2,1)S(1)}, u32[]{:S(2)}, u32[]{:S(2)}) %collective-permute-start.3) | collective-permute-done | bytes 151584 | tf_op jit(solution)/shard_map/ppermute | solution.py:380
  83.3 10.5 %collective-permute-start.9 = (bf16[544,128]{1,0:T(8,128)(2,1)S(1)}, bf16[544,128]{1,0:T(8,128)(2,1)S(1)}, u32[]{:S(2)}, u32[]{:S(2)}) collective-permute-start(bf16[544,128]{1,0:T(8,128)(2,1)S(1)} %attend_last.1), channel_id=1, source_target_pairs={{0,8},{8,0},{16,24},{24,16},{32,40},{40,32},{48,56},{56,48},{64,72... | collective-permute-start | bytes 417800 | tf_op jit(solution)/shard_map/ppermute | solution.py:388
  93.8 1.6 %attend_step.9 = (f32[512,128]{1,0:T(8,128)S(1)}, f32[512,128]{1,0:T(8,128)S(1)}, f32[512,128]{1,0:T(8,128)S(1)}) custom-call(bf16[80,1024]{1,0:T(8,128)(2,1)S(1)} %copy-done.3, bf16[2,592,128]{2,1,0:T(8,128)(2,1)S(1)} %collective-permute-done.2.refs_1_, bf16[2,592,128]{2,1,0:T(8,128)(2,1)S(1)} %collective-permute-done.6.refs_2_, ...), custom_call_target="tpu_custom_call" | custom-call | flops 1241513984 | bytes 2179072 | tf_op jit(solution)/shard_map/attend_step/pallas_call | solution.py:235
  96.9 17.7 %all_to_all.10 = bf16[8,32,1024]{2,1,0:T(8,128)(2,1)S(1)} all-to-all(bf16[8,32,1024]{2,1,0:T(8,128)(2,1)S(1)} %bitcast.13), channel_id=1, replica_groups=mesh['dp'=4,'seq'=16,'x'=4,'core'=2] {'dp','core'}, dimensions={0} | all-to-all | bytes 1048576 | tf_op jit(solution)/shard_map/all_to_all | solution.py:393
  114.6 4.2 %project.1 = bf16[4,8,32,256]{3,2,1,0:T(8,128)(2,1)S(1)} custom-call(bf16[4,2,32,1024]{3,2,1,0:T(8,128)(2,1)S(1)} %bitcast.10, bf16[1024,2048]{1,0:T(8,128)(2,1)S(1)} %copy-done, bf16[1024,2048]{1,0:T(8,128)(2,1)} %collective-permute-done.10.other_ref), custom_call_target="tpu_custom_call" | custom-call | flops 1073741824 | bytes 8388608 | tf_op jit(solution)/shard_map/project/pallas_call | solution.py:299
  118.8 17.3 %all_to_all.11 = bf16[32,32,256]{2,1,0:T(8,128)(2,1)S(1)} all-to-all(bf16[32,32,256]{2,1,0:T(8,128)(2,1)S(1)} %bitcast.11), channel_id=1, replica_groups=mesh['dp'=4,'seq'=16,'x'=4,'core'=2] {'dp','x','core'}, dimensions={0} | all-to-all | bytes 1048576 | tf_op jit(solution)/shard_map/all_to_all | solution.py:398
  (24 shorter events, 8.0 us)
Async XLA Ops:
  0.0 114.6 %collective-permute-start.10 = (bf16[1024,2048]{1,0:T(8,128)(2,1)}, bf16[1024,2048]{1,0:T(8,128)(2,1)}, u32[]{:S(2)}, u32[]{:S(2)}) collective-permute-start(bf16[1024,2048]{1,0:T(8,128)(2,1)} %own_ref.1), channel_id=1, source_target_pairs={{0,1},{1,0},{2,3},{3,2},{4,5},{5,4},{6,7},{7,6},{8,9},{9,8},{10,11... | collective-permute-start | bytes 12582920 | tf_op jit(solution)/shard_map/ppermute | solution.py:384
  11.4 15.6 %collective-permute-start.4 = (bf16[2,592,128]{2,1,0:T(8,128)(2,1)}, bf16[2,592,128]{2,1,0:T(8,128)(2,1)S(1)}, u32[]{:S(2)}, u32[]{:S(2)}) collective-permute-start(bf16[2,592,128]{2,1,0:T(8,128)(2,1)} %get-tuple-element.35.refs_1_), channel_id=1, source_target_pairs={{0,112},{8,120},{16,0},{24,8},{32,16},{40,24},{48,32},{56,40},{64,... | collective-permute-start | bytes 909320 | tf_op jit(solution)/shard_map/ppermute | solution.py:381
  17.6 19.5 %collective-permute-start = (bf16[2,592,128]{2,1,0:T(8,128)(2,1)}, bf16[2,592,128]{2,1,0:T(8,128)(2,1)S(1)}, u32[]{:S(2)}, u32[]{:S(2)}) collective-permute-start(bf16[2,592,128]{2,1,0:T(8,128)(2,1)} %get-tuple-element.35.refs_1_), channel_id=1, source_target_pairs={{0,16},{8,24},{16,32},{24,40},{32,48},{40,56},{48,64},{56,72},{64,... | collective-permute-start | bytes 909320 | tf_op jit(solution)/shard_map/ppermute | solution.py:380
  27.0 29.2 %collective-permute-start.5 = (bf16[2,592,128]{2,1,0:T(8,128)(2,1)S(1)}, bf16[2,592,128]{2,1,0:T(8,128)(2,1)S(1)}, u32[]{:S(2)}, u32[]{:S(2)}) collective-permute-start(bf16[2,592,128]{2,1,0:T(8,128)(2,1)S(1)} %collective-permute-done.4.refs_2_), channel_id=1, source_target_pairs={{0,112},{8,120},{16,0},{24,8},{32,16},{40,24},{48,32},{56,40},{64,... | collective-permute-start | bytes 909320 | tf_op jit(solution)/shard_map/ppermute | solution.py:381
  37.1 23.9 %collective-permute-start.1 = (bf16[2,592,128]{2,1,0:T(8,128)(2,1)S(1)}, bf16[2,592,128]{2,1,0:T(8,128)(2,1)S(1)}, u32[]{:S(2)}, u32[]{:S(2)}) collective-permute-start(bf16[2,592,128]{2,1,0:T(8,128)(2,1)S(1)} %collective-permute-done.refs_1_), channel_id=1, source_target_pairs={{0,16},{8,24},{16,32},{24,40},{32,48},{40,56},{48,64},{56,72},{64,... | collective-permute-start | bytes 909320 | tf_op jit(solution)/shard_map/ppermute | solution.py:380
  39.0 15.9 %collective-permute-start.8 = (bf16[80,1024]{1,0:T(8,128)(2,1)}, bf16[80,1024]{1,0:T(8,128)(2,1)S(1)}, u32[]{:S(2)}, u32[]{:S(2)}) collective-permute-start(bf16[80,1024]{1,0:T(8,128)(2,1)} %get-tuple-element.34.refs_0_), channel_id=1, source_target_pairs={{0,8},{8,0},{16,24},{24,16},{32,40},{40,32},{48,56},{56,48},{64,72... | collective-permute-start | bytes 491528 | tf_op jit(solution)/shard_map/ppermute | solution.py:383
  41.4 1.0 copy-start.1
  42.4 0.9 copy-start.2
  43.3 21.2 %copy-start.3 = (bf16[80,1024]{1,0:T(8,128)(2,1)S(1)}, bf16[80,1024]{1,0:T(8,128)(2,1)}, u32[]{:S(2)}) copy-start(bf16[80,1024]{1,0:T(8,128)(2,1)} %get-tuple-element.34.refs_0_) | copy-start | bytes 491524
  56.2 11.5 %collective-permute-start.6 = (bf16[2,592,128]{2,1,0:T(8,128)(2,1)S(1)}, bf16[2,592,128]{2,1,0:T(8,128)(2,1)S(1)}, u32[]{:S(2)}, u32[]{:S(2)}) collective-permute-start(bf16[2,592,128]{2,1,0:T(8,128)(2,1)S(1)} %collective-permute-done.5.refs_2_), channel_id=1, source_target_pairs={{0,112},{8,120},{16,0},{24,8},{32,16},{40,24},{48,32},{56,40},{64,... | collective-permute-start | bytes 909320 | tf_op jit(solution)/shard_map/ppermute | solution.py:381
  61.0 12.2 %collective-permute-start.2 = (bf16[2,592,128]{2,1,0:T(8,128)(2,1)S(1)}, bf16[2,592,128]{2,1,0:T(8,128)(2,1)S(1)}, u32[]{:S(2)}, u32[]{:S(2)}) collective-permute-start(bf16[2,592,128]{2,1,0:T(8,128)(2,1)S(1)} %collective-permute-done.1.refs_1_), channel_id=1, source_target_pairs={{0,16},{8,24},{16,32},{24,40},{32,48},{40,56},{48,64},{56,72},{64,... | collective-permute-start | bytes 909320 | tf_op jit(solution)/shard_map/ppermute | solution.py:380
  67.7 10.6 %collective-permute-start.7 = (bf16[1,592,128]{2,1,0:T(8,128)(2,1)S(1)}, bf16[1,592,128]{2,1,0:T(8,128)(2,1)S(1)}, u32[]{:S(2)}, u32[]{:S(2)}) collective-permute-start(bf16[1,592,128]{2,1,0:T(8,128)(2,1)S(1)} %slice.9), channel_id=1, source_target_pairs={{0,112},{8,120},{16,0},{24,8},{32,16},{40,24},{48,32},{56,40},{64,... | collective-permute-start | bytes 454664 | tf_op jit(solution)/shard_map/ppermute | solution.py:381
  73.2 8.8 %collective-permute-start.3 = (bf16[1,592,128]{2,1,0:T(8,128)(2,1)S(1)}, bf16[1,592,128]{2,1,0:T(8,128)(2,1)S(1)}, u32[]{:S(2)}, u32[]{:S(2)}) collective-permute-start(bf16[1,592,128]{2,1,0:T(8,128)(2,1)S(1)} %slice.8), channel_id=1, source_target_pairs={{0,16},{8,24},{16,32},{24,40},{32,48},{40,56},{48,64},{56,72},{64,... | collective-permute-start | bytes 454664 | tf_op jit(solution)/shard_map/ppermute | solution.py:380
  83.3 13.4 %collective-permute-start.9 = (bf16[544,128]{1,0:T(8,128)(2,1)S(1)}, bf16[544,128]{1,0:T(8,128)(2,1)S(1)}, u32[]{:S(2)}, u32[]{:S(2)}) collective-permute-start(bf16[544,128]{1,0:T(8,128)(2,1)S(1)} %attend_last.1), channel_id=1, source_target_pairs={{0,8},{8,0},{16,24},{24,16},{32,40},{40,32},{48,56},{56,48},{64,72... | collective-permute-start | bytes 417800 | tf_op jit(solution)/shard_map/ppermute | solution.py:388
  93.8 20.8 %copy-start = (bf16[1024,2048]{1,0:T(8,128)(2,1)S(1)}, bf16[1024,2048]{1,0:T(8,128)(2,1)}, u32[]{:S(2)}) copy-start(bf16[1024,2048]{1,0:T(8,128)(2,1)} %own_ref.1) | copy-start | bytes 12582916
